TPU v7x, 256 devices: a 2x2x32 block of a 4x8x32 slice. The times are simulated.
256 devices in a mesh: event: 4 (over y, x), draw: 32 (over z), bin: 2 (over core).
Axes of the slice: x: 2, y: 2, z: 32, core: 2. Of those that a mesh axis runs over, the one named last changes fastest.
The devices are a block of a 4x8x32 slice.
Arguments:
- fine_cross: float32 [12, 2, 8192], P('event', None, 'draw'), parts along dimension 0, may hold values from -0.15 to 0.15
- fine_power: float32 [12, 8192], P('event', 'draw'), parts along dimension 0, may hold values from 0.000125 to 0.005
- bin_widths: int32 [512], P('event'), parts along dimension 0, may hold values from 1 to 128, 8192 in all
- log_amps: float32 [12, 32768], P('event', 'draw'), parts along dimension 0, may hold values from -0.5 to 0.5
- delays: float32 [12, 32768], P('event', 'draw'), parts along dimension 0, may hold values from -1.5 to 1.5
- phases: float32 [131072], P(('event', 'draw')), parts along dimension 0, may hold values from -3.140625 to 3.140625
- chirps: float32 [131072], P(('event', 'draw')), parts along dimension 0, may hold values from -8 to 8
- proposal_log: float32 [131072], P(('event', 'draw')), parts along dimension 0, may hold values from -100 to 130
Outputs:
- log_weights: float32 [131072], P(('event', 'draw')), parts along dimension 0
- log_evidence: float32 [4], P('event'), parts along dimension 0
There are 4 independent parts, one for each index of `event`. A program takes and returns all parts, laid end to end along the dimension named above; each array names one. Nothing has to cross between parts.
Inputs may be any that keep to these rules, and one draw needn't show every extreme that they name: `bin_widths`: the widths of an event sum to 8192; each is 1 to 128 and one is exactly 128.
All inputs are finite; a program needn't handle non-finite values.
Results may differ from a plain program's by a relative error of at most 0.00016.
Values sent between devices are 32-bit elements; how exact they have to be, the bound alone decides.
No kernel may reach another device: no remote copies, remote signals or barrier semaphores. Data moves between devices by JAX's collectives and lax.ppermute only.
A program may use at most 64 MiB of HBM per device.

v0:
```python
import math

import jax
import jax.numpy as jnp
from jax import lax
from jax.sharding import PartitionSpec as P

FINE = 8192
TSHIFT = 2048


TWO_PI = 2.0 * math.pi
TIME_STEP = 0.125
PRECISE = lax.Precision.HIGHEST


def copy_for_each(array, axis):
    count = lax.axis_size(axis)
    return lax.all_to_all(
        jnp.broadcast_to(array[None], (count, *array.shape)), axis, 0, 0, tiled=True
    )


def of_everyone(array, axis):
    everything = copy_for_each(array, axis)
    return jnp.sum(everything, axis=0)


def together(arrays, axis):
    line, at, finished = (jnp.concatenate([a.reshape(-1) for a in arrays]), 0, [])
    running = of_everyone(line, axis)
    for a in arrays:
        finished.append(running[at : at + a.size].reshape(a.shape))
        at += a.size
    return tuple(finished)


def gathered_once(array, axis):
    leaves = jax.tree.leaves(array)
    sequence = sorted(range(len(leaves)), key=lambda k: -leaves[k].size)
    width = (1, *leaves[sequence[0]].shape)[-1]
    lines = [
        jnp.pad(leaves[k].reshape(-1), (0, -leaves[k].size % width)).reshape(-1, width)
        for k in sequence
    ]
    both, at, found = (copy_for_each(jnp.concatenate(lines), axis), 0, {})
    for k, line in zip(sequence, lines):
        piece = both[:, at : at + len(line)].reshape(len(both), -1)
        found[k] = piece[:, : leaves[k].size].reshape(-1, *leaves[k].shape)
        at += len(line)
    numbers = iter(range(len(leaves)))
    return jax.tree.map(lambda _: found[next(numbers)], array)


def joined_by_halves(pieces, combine):
    while len(jax.tree.leaves(pieces)[0]) > 1:
        pieces = jax.vmap(combine)(
            *(jax.tree.map(lambda part: part[side::2], pieces) for side in (0, 1))
        )
    return jax.tree.map(lambda part: part[0], pieces)


def merged(array, axis, combine):
    pieces = gathered_once(array, axis)
    return joined_by_halves(pieces, combine)


def summary_terms(cross_rows, power_rows, first_fine, lower_edge, bin_widths):
    fine_index = first_fine + jnp.arange(power_rows.shape[1], dtype=jnp.int32)
    upper_edge = lower_edge + bin_widths
    inside = (
        (fine_index[:, None] >= lower_edge[None, :]) & (fine_index[:, None] < upper_edge[None, :])
    ).astype(jnp.float32)
    offset = fine_index.astype(jnp.float32)[:, None] + 0.5 - lower_edge.astype(jnp.float32)[None, :]
    weight = inside * offset / bin_widths.astype(jnp.float32)[None, :]
    lower_weight = inside - weight
    detectors = power_rows.shape[0]
    flattened = cross_rows.reshape(detectors * 2, -1)
    start_sums = jnp.dot(flattened, lower_weight, precision=PRECISE).reshape(detectors, 2, -1)
    end_sums = jnp.dot(flattened, weight, precision=PRECISE).reshape(detectors, 2, -1)
    power_low = jnp.dot(power_rows, lower_weight * lower_weight, precision=PRECISE)
    power_mixed = jnp.dot(power_rows, lower_weight * weight, precision=PRECISE)
    power_high = jnp.dot(power_rows, weight * weight, precision=PRECISE)
    return (start_sums, end_sums, power_low, power_mixed, power_high)


def edge_phase(freq_values, delays, phases, chirps):
    return (
        (TWO_PI * freq_values)[None, :, None] * delays[:, None, :]
        + phases[None, None, :]
        + chirps[None, None, :] * (freq_values * freq_values)[None, :, None]
    )


def sample_terms(
    freq_low, freq_high, log_amps, delays, phases, chirps, power_low, power_mixed, power_high
):
    amplitude = jnp.exp(log_amps)[:, None, :]
    phase_low = edge_phase(freq_low, delays, phases, chirps)
    phase_high = edge_phase(freq_high, delays, phases, chirps)
    pair_low = jnp.stack([amplitude * jnp.cos(phase_low), amplitude * jnp.sin(phase_low)], axis=2)
    pair_high = jnp.stack(
        [amplitude * jnp.cos(phase_high), amplitude * jnp.sin(phase_high)], axis=2
    )
    features = jnp.stack([pair_low, pair_high], axis=2).reshape(-1, log_amps.shape[1])
    cos_diff = jnp.cos(phase_low - phase_high)
    inner_sum = jnp.sum(power_low + power_high, axis=1)[:, None] + 2.0 * jnp.einsum(
        "db,dbn->dn", power_mixed, cos_diff, precision=PRECISE
    )
    self_power = jnp.sum(jnp.exp(2.0 * log_amps) * inner_sum, axis=0)
    return (features, self_power)


def build_table(row_count, total_shifts, start_sums, end_sums, freq_low, freq_high):
    shifts = (jnp.arange(row_count, dtype=jnp.int32) - total_shifts // 2).astype(
        jnp.float32
    ) * TIME_STEP
    edge_freq = jnp.stack([freq_low, freq_high], axis=-1)
    angles = (TWO_PI * edge_freq)[None] * shifts[:, None, None]
    cosine = jnp.cos(angles)[:, None]
    sine_value = jnp.sin(angles)[:, None]
    real_part = jnp.stack([start_sums[:, 0], end_sums[:, 0]], axis=-1)[None]
    imag_part = jnp.stack([start_sums[:, 1], end_sums[:, 1]], axis=-1)[None]
    table_real = real_part * cosine + imag_part * sine_value
    table_imag = imag_part * cosine - real_part * sine_value
    return jnp.stack([table_real, table_imag], axis=-1).reshape(row_count, -1)


def merge_stats(first_stats, second_stats):
    largest = jnp.maximum(first_stats[0], second_stats[0])
    return (
        largest,
        first_stats[1] * jnp.exp(first_stats[0] - largest)
        + second_stats[1] * jnp.exp(second_stats[0] - largest),
    )


def column_lse(scores):
    largest = jnp.max(scores, axis=0)
    return largest + jnp.log(jnp.sum(jnp.exp(scores - largest[None, :]), axis=0)) - math.log(TSHIFT)


def body(fine_cross, fine_power, bin_widths, log_amps, delays, phases, chirps, proposal_log):
    fine_count = fine_power.shape[1]
    first_fine = lax.axis_index("draw") * fine_count
    upper_edge = jnp.cumsum(bin_widths)
    lower_edge = upper_edge - bin_widths
    sample_count = log_amps.shape[1] // lax.axis_size("bin")
    sample_start = lax.axis_index("bin") * sample_count
    log_amps = lax.dynamic_slice_in_dim(log_amps, sample_start, sample_count, 1)
    delays = lax.dynamic_slice_in_dim(delays, sample_start, sample_count, 1)
    phases = lax.dynamic_slice_in_dim(phases, sample_start, sample_count, 0)
    chirps = lax.dynamic_slice_in_dim(chirps, sample_start, sample_count, 0)
    proposal_log = lax.dynamic_slice_in_dim(proposal_log, sample_start, sample_count, 0)
    upper_edge = lower_edge + bin_widths
    local_sums = summary_terms(fine_cross, fine_power, first_fine, lower_edge, bin_widths)
    start_sums, end_sums, power_low, power_mixed, power_high = together(
        (local_sums[0], local_sums[1], local_sums[2], local_sums[3], local_sums[4]), "draw"
    )
    freq_low = lower_edge.astype(jnp.float32) / FINE
    freq_high = upper_edge.astype(jnp.float32) / FINE
    features, self_power = sample_terms(
        freq_low, freq_high, log_amps, delays, phases, chirps, power_low, power_mixed, power_high
    )
    matrix = build_table(TSHIFT, TSHIFT, start_sums, end_sums, freq_low, freq_high)
    cross_terms = jnp.dot(matrix, features, precision=PRECISE)
    partial_value = cross_terms - 0.5 * self_power[None, :]
    scores = partial_value + proposal_log[None, :]
    marginal = lax.all_gather(column_lse(scores), "bin", axis=0, tiled=True)
    local_top = jnp.max(marginal)
    local_sum = jnp.sum(jnp.exp(marginal - local_top))
    largest, summed = merged((local_top, local_sum), "draw", merge_stats)
    total_log = largest + jnp.log(summed)
    total_draws = marginal.shape[0] * lax.axis_size("draw")
    return (marginal - total_log, (total_log - math.log(total_draws)).reshape(1))


def solution(mesh):
    placed = (
        P("event", None, "draw"),
        P("event", "draw"),
        P("event"),
        P("event", "draw"),
        P("event", "draw"),
        P(("event", "draw")),
        P(("event", "draw")),
        P(("event", "draw")),
    )
    return jax.shard_map(
        body,
        mesh=mesh,
        in_specs=placed,
        out_specs=(P(("event", "draw")), P("event")),
        check_vma=False,
    )
```

profile of v0, /device:TPU:37, one launch (start us, length us, event | category | flops | bytes accessed | tf_op | source)
XLA Modules:
  0.0 164.6 jit_solution(7765121159152370908)
XLA Ops:
  0.6 0.0 copy-start
  0.6 0.0 copy-start.3
  0.7 0.0 copy-start.4
  0.7 0.0 copy-start.5
  0.7 0.7 convert_element_type.48
  1.4 0.8 copy.39
  2.1 0.2 reduce-window.4
  2.3 0.1 reduce.3
  2.4 0.7 convert_multiply_fusion.1
  3.1 0.7 reshape.273
  3.8 0.3 convolution_bitcast_fusion.1
  4.1 0.3 convolution_bitcast_fusion
  4.4 1.0 convolution_bitcast_fusion.4
  5.4 1.0 convolution_bitcast_fusion.3
  6.3 1.0 convolution_bitcast_fusion.2
  7.3 0.0 copy-start.2
  7.4 0.9 broadcast_in_dim.6
  8.3 33.2 %all-to-all-start = ((f32[32,1,2688]{2,1,0:T(1,128)}), f32[32,1,2688]{2,1,0:T(1,128)S(1)}, u32[]{:S(2)}, u32[]{:S(2)}) async-start(f32[32,1,2688]{2,1,0:T(1,128)} %broadcast_in_dim.6), calls=%async_computation | async-start | bytes 688128 | tf_op jit(solution)/shard_map/all_to_all | solution.py:19
  41.6 0.1 copy.41
  41.6 0.0 copy-done.3
  41.6 0.1 dynamic_slice.18
  41.7 0.0 copy-done.4
  41.7 0.1 dynamic_slice.17
  41.8 0.0 copy-done.5
  41.8 0.1 dynamic_slice.19
  41.9 0.0 copy-done
  41.9 0.1 broadcast_multiply_fusion.1
  42.0 8.7 %multiply_cosine_fusion = (f32[2048,128,2]{1,0,2:T(8,128)S(1)}, f32[2048,128,2]{1,0,2:T(8,128)}) fusion(f32[2048]{0:T(1024)S(1)} %convert_multiply_fusion, f32[128,2]{0,1:T(2,128)S(1)} %maximum_multiply_fusion), kind=kLoop, calls=%fused_computation.14 | loop fusion | flops 524288 | bytes 4203520 | tf_op jit(solution)/shard_map/cos | solution.py:120
  50.7 38.3 %all-to-all-done = f32[32,1,2688]{2,1,0:T(1,128)S(1)} async-done(((f32[32,1,2688]{2,1,0:T(1,128)}), f32[32,1,2688]{2,1,0:T(1,128)S(1)}, u32[]{:S(2)}, u32[]{:S(2)}) %all-to-all-start) | async-done | bytes 344096 | tf_op jit(solution)/shard_map/all_to_all | solution.py:19
  89.1 0.2 reduce_sum.45
  89.3 0.1 fusion.31
  89.4 0.0 copy-start.1
  89.5 3.2 %fusion.9 = f32[3,1,512]{2,1,0:T(1,128)S(1)} fusion(f32[128,512]{1,0:T(8,128)S(1)} %get-tuple-element.33, f32[128]{0:T(128)S(1)} %get-tuple-element.40, f32[128,512]{1,0:T(8,128)S(1)} %get-tuple-element.32, f32[512]{0:T(512)S(1)} %dynamic_slice.17, f32[3,512]{1,0:T(4,128)S(1)} %constant_dynamic-slice_fusion, f32[128]{0:T(128)S(1)} %get-tuple-element.42, ...), kind=kOutput, calls=%fused_computation.22 | convolution fusion | flops 3735552 | bytes 541184 | tf_op jit(solution)/shard_map/db,dbn->dn/dot_general | solution.py:107
  92.7 0.1 fusion.29
  92.8 6.8 %cosine_multiply_fusion.1 = (f32[3,128,1,512]{3,1,2,0:T(8,128)S(1)}, f32[3,128,1,512]{3,1,2,0:T(8,128)S(1)}, f32[3,128,1,512]{3,1,2,0:T(8,128)}, f32[3,128,1,512]{3,1,2,0:T(8,128)}) fusion(f32[128,512]{1,0:T(8,128)S(1)} %get-tuple-element.32, f32[512]{0:T(512)S(1)} %dynamic_slice.17, f32[3,512]{1,0:T(4,128)S(1)} %constant_dynamic-slice_fusion, ...), kind=kLoop, calls=%fused_computation.35 | loop fusion | flops 1966080 | bytes 3685376 | tf_op jit(solution)/shard_map/mul | solution.py:101
  99.6 1.6 multiply_add_fusion
  101.1 1.7 %maximum_bitcast_fusion = (f32[3,128,1,2,512]{4,1,3,2,0:T(8,128)S(1)}, f32[3,128,1,2,512]{4,1,3,2,0:T(8,128)S(1)}) fusion(f32[3,128,1,512]{3,1,2,0:T(8,128)S(1)} %get-tuple-element.17, f32[3,128,1,512]{3,1,2,0:T(8,128)S(1)} %get-tuple-element.16, f32[3,128,1,512]{3,1,2,0:T(8,128)} %get-tuple-element.20, f32[3,128,1,512]{3,1,2,0:T(8,128)} %get-tuple-element.21), kind=kLoop, calls=%fused_computation.15 | loop fusion | flops 786432 | bytes 6291456 | tf_op jit(solution)/shard_map/stack | solution.py:105
  102.8 20.2 %fusion.5 = (f32[512]{0:T(512)S(1)}, f32[2048,512,1,1,1]{1,0,4,3,2:T(8,128)S(1)}) fusion(f32[512]{0:T(512)S(1)} %dynamic_slice.19, f32[512]{0:T(512)S(1)} %broadcast_multiply_fusion.2, f32[3,128,1,2,512]{4,1,3,2,0:T(8,128)S(1)} %get-tuple-element.47, f32[3,128,1,2,512]{4,1,3,2,0:T(8,128)S(1)} %get-tuple-element.46, ...), kind=kOutput, calls=%fused_computation.9 | convolution fusion | flops 19334430720 | bytes 19929088 | tf_op jit(solution)/shard_map/dot_general | solution.py:166
  123.0 0.9 exponential_reduce_fusion
  123.9 3.9 %all-gather = f32[2,1,512]{2,1,0:T(1,128)S(1)} all-gather(f32[1,1,512]{2,1,0:T(1,128)S(1)} %bitcast.76), channel_id=1, replica_groups=mesh['event'=4,'draw'=32,'bin'=2] {'bin'}, dimensions={0}, use_global_device_ids=true | all-gather | bytes 6144 | tf_op jit(solution)/shard_map/all_gather | solution.py:169
  127.9 0.6 reduce_max.19
  128.5 1.3 exponential_reduce_fusion.1
  129.7 1.4 maximum_bitcast_fusion.2
  131.1 24.4 %all_to_all.11 = f32[32,2,1]{1,2,0:T(1,128)S(1)} all-to-all(f32[32,2,1]{1,2,0:T(1,128)S(1)} %broadcast_in_dim.8), channel_id=1, replica_groups=mesh['event'=4,'draw'=32,'bin'=2] {'draw'}, dimensions={0} | all-to-all | bytes 512 | tf_op jit(solution)/shard_map/all_to_all | solution.py:19
  155.5 0.6 slice_reduce_fusion
  156.0 0.1 slice.134
  156.1 0.1 slice.135
  156.3 0.1 slice.145
  156.4 0.1 slice.146
  156.5 0.1 slice.136
  156.6 0.1 slice.137
  156.7 0.1 slice.147
  156.8 0.1 slice.148
  156.9 0.1 slice.138
  157.0 0.1 slice.139
  157.1 0.1 slice.149
  157.2 0.1 slice.150
  157.3 0.1 slice.140
  157.4 0.1 slice.141
  157.5 0.1 slice.151
  157.6 0.1 slice.152
  157.7 0.6 fusion.36
  160.9 0.6 fusion.35
  162.9 0.6 broadcast_subtract_fusion
  (30 shorter events, 0.2 us)
Async XLA Ops:
  0.6 41.3 %copy-start = (f32[3,1024]{1,0:T(4,128)S(1)}, f32[3,1024]{1,0:T(4,128)}, u32[]{:S(2)}) copy-start(f32[3,1024]{1,0:T(4,128)} %param.12) | copy-start | bytes 36868
  0.6 41.0 %copy-start.3 = (f32[1024]{0:T(1024)S(1)}, f32[1024]{0:T(1024)}, u32[]{:S(2)}) copy-start(f32[1024]{0:T(1024)} %param.14) | copy-start | bytes 12292
  0.7 41.1 %copy-start.4 = (f32[1024]{0:T(1024)S(1)}, f32[1024]{0:T(1024)}, u32[]{:S(2)}) copy-start(f32[1024]{0:T(1024)} %param.13) | copy-start | bytes 12292
  0.7 41.1 %copy-start.5 = (f32[1024]{0:T(1024)S(1)}, f32[1024]{0:T(1024)}, u32[]{:S(2)}) copy-start(f32[1024]{0:T(1024)} %param.15) | copy-start | bytes 12292
  7.3 85.4 %copy-start.2 = (f32[3,1024]{1,0:T(4,128)S(1)}, f32[3,1024]{1,0:T(4,128)}, u32[]{:S(2)}) copy-start(f32[3,1024]{1,0:T(4,128)} %param.11) | copy-start | bytes 36868
  8.3 80.7 %all-to-all-start = ((f32[32,1,2688]{2,1,0:T(1,128)}), f32[32,1,2688]{2,1,0:T(1,128)S(1)}, u32[]{:S(2)}, u32[]{:S(2)}) async-start(f32[32,1,2688]{2,1,0:T(1,128)} %broadcast_in_dim.6), calls=%async_computation | async-start | bytes 688128 | tf_op jit(solution)/shard_map/all_to_all | solution.py:19
  89.4 10.1 %copy-start.1 = (f32[2048,128,2]{1,0,2:T(8,128)S(1)}, f32[2048,128,2]{1,0,2:T(8,128)}, u32[]{:S(2)}) copy-start(f32[2048,128,2]{1,0,2:T(8,128)} %get-tuple-element.27) | copy-start | bytes 6291460
where the time goes:
time: 165 us
  waiting for transfers between devices  38.3 us (23%)
  starting transfers between devices  33.2 us (20%)
  blocking collectives  28.3 us (17%)
  matrix products  26.9 us (16%)
  other arithmetic  25.7 us (16%)
  local copies, waits for them, and re-layouts  6.13 us (4%)
  between operations  6.07 us (4%)
    all_to_all x1, waiting for transfers between devices, copy_for_each(): lax.all_to_all(jnp.broadcast_to(array[None], (count, *array.shape)), axis...  38.3 us
    all_to_all x1, starting transfers between devices, copy_for_each(): lax.all_to_all(jnp.broadcast_to(array[None], (count, *array.shape)), axis...  33.2 us
    all_to_all x1, blocking collectives, copy_for_each(): lax.all_to_all(jnp.broadcast_to(array[None], (count, *array.shape)), axis...  24.4 us
    dot_general x1, matrix products, body(): cross_terms = jnp.dot(matrix, features, precision=PRECISE)  20.2 us
    cos x1, other arithmetic, build_table(): cosine = jnp.cos(angles)[:, None]  8.71 us
    mul x1, other arithmetic, sample_terms(): amplitude * jnp.cos(phase_low)  6.77 us
    all_gather x1, blocking collectives, body(): marginal = lax.all_gather(column_lse(scores), 'bin', axis=0, tiled=True)  3.95 us
  transfers between devices with their start and end apart: 1, of which 1 were waited for; matrix products, arithmetic and copies ran while one was open for 6% of the time, Pallas kernels for 0%

commit v1 on v0

v1 whole, which is shorter than its diff:
```python
import math

import jax
import jax.numpy as jnp
import numpy as np
from jax import lax
from jax.experimental import pallas as pl
from jax.experimental.pallas import tpu as pltpu
from jax.sharding import PartitionSpec as P

TSHIFT = 2048
TIME_STEP = 0.125
CHUNK = 256
LANES = 128
ROWS = 5
VMEM = pl.BlockSpec(memory_space=pltpu.VMEM)
F32, BF16 = jnp.float32, jnp.bfloat16


def fit(function, terms):
    nodes = 0.125 * (1.0 + np.cos((np.arange(64) + 0.5) * np.pi / 64))
    basis = np.vander(nodes / 0.25, terms, increasing=True)
    found = np.linalg.lstsq(basis, function(np.sqrt(nodes)), rcond=None)[0]
    return [float(c) for c in found / 0.25 ** np.arange(terms)]


COS = fit(lambda r: np.cos(2 * np.pi * r), 9)
SIN = fit(lambda r: np.sin(2 * np.pi * r) / r, 9)


def horner(coefficients, x):
    total = jnp.full_like(x, coefficients[-1])
    for c in coefficients[-2::-1]:
        total = total * x + c
    return total


def turn(u):
    r = u - jnp.round(u)
    square = r * r
    return horner(COS, square), horner(SIN, square) * r


def call(kernel, outs, *args, limit=24 << 20, flops=1 << 20, name=None):
    return pl.pallas_call(
        kernel,
        out_shape=outs,
        in_specs=[VMEM] * len(args),
        out_specs=jax.tree.map(lambda _: VMEM, outs),
        compiler_params=pltpu.CompilerParams(vmem_limit_bytes=limit),
        cost_estimate=pl.CostEstimate(flops=flops, bytes_accessed=1 << 20, transcendentals=0),
        name=name,
    )(*args)


def edges(widths):
    wide = widths.astype(F32)
    bins = wide.shape[1]
    before = lax.broadcasted_iota(jnp.int32, (bins, bins), 0)
    mine = lax.broadcasted_iota(jnp.int32, (bins, bins), 1)
    ones = jnp.where(before <= mine, 1.0, 0.0).astype(BF16)
    rows = jnp.broadcast_to(wide, (16, bins)).astype(BF16)
    upper = jnp.dot(rows, ones, preferred_element_type=F32)[:1]
    return wide, upper


def split(x):
    high = x.astype(BF16)
    return high, (x - high.astype(F32)).astype(BF16)


def summary_kernel(cross_ref, power_ref, widths_ref, out_ref):
    fine, bins = power_ref.shape[1], widths_ref.shape[1]
    wide, upper = edges(widths_ref[...])
    lower = upper - wide
    first = (lax.axis_index("draw") * fine).astype(F32)
    at = lax.broadcasted_iota(jnp.int32, (fine, bins), 0).astype(F32) + first
    inside = (at >= lower) & (at < upper)
    up = jnp.where(inside, 2.0 * (at - lower) + 1.0, 0.0)
    down = jnp.where(inside, 2.0 * wide - up, 0.0)
    both_high, both_low = split(up * down)
    weights = jnp.concatenate([up.astype(BF16), down.astype(BF16), both_high, both_low], axis=1)
    data = jnp.concatenate(
        [cross_ref[...], power_ref[...], jnp.zeros((7, fine), F32)], axis=0
    )
    high = data.astype(BF16)
    rest = data - high.astype(F32)
    middle, low = split(rest)
    got = jnp.dot(
        jnp.concatenate([high, middle, low], axis=0), weights, preferred_element_type=F32
    )
    got = got[:16] + got[16:32] + got[32:]
    scale = 0.5 / wide
    end = got[:, :bins] * scale
    start = got[:, bins : 2 * bins] * scale
    mixed = (got[:, 2 * bins : 3 * bins] + got[:, 3 * bins :]) * (scale * scale)
    row = lax.broadcasted_iota(jnp.int32, (16, bins), 0)
    lane = lax.broadcasted_iota(jnp.int32, (16, bins), 1)
    merged = end + jnp.where(lane < bins - 1, pltpu.roll(start, bins - 1, 1), 0.0)
    total = jnp.sum(data, axis=1, keepdims=True)
    single = jnp.where(row < 6, start[:, :1], total)
    single = jnp.sum(jnp.where(lane == row, single, 0.0), axis=0, keepdims=True)
    table = jnp.where(row < 6, merged, mixed)
    table = jnp.where(row == 9, single, table)
    mine = lax.axis_index("bin")
    for r in range(ROWS):
        line = jnp.where(mine == 0, table[r : r + 1], table[ROWS + r : ROWS + r + 1])
        out_ref[:, :, r * bins : (r + 1) * bins] = jnp.broadcast_to(
            line[None], (out_ref.shape[0], 1, bins)
        )


def terms_kernel(
    widths_ref, amps_ref, delays_ref, phases_ref, chirps_ref, prior_ref,
    high_ref, low_ref, features_ref, spread_ref, flat_ref, grid=0.0,
):
    wide, upper = edges(widths_ref[...])
    bins = wide.shape[1]
    draws = features_ref.shape[2]
    mine = pl.ds(pl.multiple_of(lax.axis_index("bin") * draws, draws), draws)
    for c in range(TSHIFT // CHUNK):
        shift = lax.broadcasted_iota(jnp.int32, (CHUNK, bins), 0).astype(F32)
        shift = shift + float(c * CHUNK - TSHIFT // 2)
        cosine, sine = turn((shift * upper) * (TIME_STEP / grid))
        rows = slice(c * CHUNK, (c + 1) * CHUNK)
        high_ref[rows, :bins], low_ref[rows, :bins] = split(cosine)
        high_ref[rows, bins:], low_ref[rows, bins:] = split(sine)
    tall = jnp.concatenate(
        [wide, upper, jnp.zeros((bins - 2, bins), F32)], axis=0
    ).T
    width, x = tall[:, :1] * (1.0 / grid), tall[:, 1:2] * (1.0 / grid)
    phases, chirps = phases_ref[:, mine], chirps_ref[:, mine]
    base = phases * (0.5 / math.pi)
    bend = chirps * (0.5 / math.pi)
    common = base + bend * (x * x)
    half_bend = (0.5 * width * (x + (x - width))) * chirps
    cos0, sin0 = turn(base)
    for d in range(3):
        amp = jnp.exp(amps_ref[d : d + 1, mine])
        delay = delays_ref[d : d + 1, mine]
        cosine, sine = turn(x * delay + common)
        features_ref[2 * d] = amp * cosine
        features_ref[2 * d + 1] = amp * sine
        half = (math.pi * width) * delay + half_bend
        h2 = half * half
        sh = half * (1.0 + h2 * (-1.0 / 6 + h2 * (1.0 / 120 + h2 * (-1.0 / 5040))))
        spread_ref[d] = (2.0 * amp * sh) * (amp * sh)
        flat_ref[2 * d : 2 * d + 1] = amp * cos0
        flat_ref[2 * d + 1 : 2 * d + 2] = amp * sin0
        flat_ref[6 + d : 7 + d] = (-0.5 * amp) * amp
    flat_ref[9:10] = prior_ref[:, mine]


def score_kernel(sums_ref, high_ref, low_ref, features_ref, spread_ref, flat_ref, out_ref, stat_ref):
    bins = features_ref.shape[1]
    draws = features_ref.shape[2]
    lines = [
        sums_ref[r // ROWS, :, (r % ROWS) * bins : (r % ROWS + 1) * bins] for r in range(2 * ROWS)
    ]
    single = lines[9]
    tall = jnp.concatenate(lines[:9] + [jnp.zeros((bins - 9, bins), F32)], axis=0).T
    real = imag = power = None
    offset = flat_ref[9:10]
    for d in range(3):
        a, b, mixed = tall[:, 2 * d : 2 * d + 1], tall[:, 2 * d + 1 : 2 * d + 2], tall[:, 6 + d : 7 + d]
        cosine, sine = features_ref[2 * d], features_ref[2 * d + 1]
        re, im, pw = a * cosine + b * sine, b * cosine - a * sine, mixed * spread_ref[d]
        real = re if real is None else real + re
        imag = im if imag is None else imag + im
        power = pw if power is None else power + pw
        offset = (
            offset
            + single[:, 2 * d : 2 * d + 1] * flat_ref[2 * d : 2 * d + 1]
            + single[:, 2 * d + 1 : 2 * d + 2] * flat_ref[2 * d + 1 : 2 * d + 2]
            + single[:, 6 + d : 7 + d] * flat_ref[6 + d : 7 + d]
        )
    offset = offset + jnp.sum(power, axis=0, keepdims=True)
    wide_high, wide_low = split(jnp.concatenate([real, imag], axis=0))
    top = total = None
    for c in range(TSHIFT // CHUNK):
        rows = slice(c * CHUNK, (c + 1) * CHUNK)
        high, low = high_ref[rows, :], low_ref[rows, :]
        cross = (
            jnp.dot(high, wide_high, preferred_element_type=F32)
            + jnp.dot(high, wide_low, preferred_element_type=F32)
            + jnp.dot(low, wide_high, preferred_element_type=F32)
        )
        cross = cross.reshape(CHUNK // 8, 8, draws)
        peak = jnp.max(cross, axis=0)
        if top is not None:
            peak = jnp.maximum(peak, top)
            total = total * jnp.exp(top - peak)
        add = jnp.sum(jnp.exp(cross - peak[None]), axis=0)
        total = add if total is None else total + add
        top = peak
    peak = jnp.max(top, axis=0, keepdims=True)
    total = jnp.sum(total * jnp.exp(top - peak), axis=0, keepdims=True)
    marginal = (peak + jnp.log(total) - math.log(TSHIFT)) + offset
    out_ref[...] = marginal
    best = jnp.max(marginal, axis=1, keepdims=True)
    mass = jnp.sum(jnp.exp(marginal - best), axis=1, keepdims=True)
    lane = lax.broadcasted_iota(jnp.int32, (1, LANES), 1)
    stat = jnp.where(lane == 0, best, mass)
    stat_ref[...] = jnp.broadcast_to(stat[None], stat_ref.shape)


def final_kernel(stats_ref, marginal_ref, out_ref, evidence_ref, draws=0):
    stats = stats_ref[...]
    best, mass = stats[:, :, :1], stats[:, :, 1:2]
    top = jnp.max(best, axis=0, keepdims=True)
    total = top + jnp.log(jnp.sum(mass * jnp.exp(best - top), axis=0, keepdims=True))
    out_ref[...] = marginal_ref[...] - total
    evidence_ref[...] = total[0] - math.log(draws)


def body(fine_cross, fine_power, bin_widths, log_amps, delays, phases, chirps, proposal_log):
    shards, cores = lax.axis_size("draw"), lax.axis_size("bin")
    detectors, fine = fine_power.shape
    bins = bin_widths.shape[0]
    whole = log_amps.shape[1]
    draws = whole // cores
    widths = bin_widths.reshape(1, bins)
    sums = call(
        summary_kernel,
        jax.ShapeDtypeStruct((shards, 1, ROWS * bins), F32),
        fine_cross.reshape(2 * detectors, fine), fine_power, widths,
        flops=1 << 24, name="summary",
    )
    everyone = lax.all_to_all(sums, "draw", 0, 0, tiled=True)
    high, low, features, spread, flat = call(
        lambda *refs: terms_kernel(*refs, grid=float(fine * shards)),
        (
            jax.ShapeDtypeStruct((TSHIFT, 2 * bins), BF16),
            jax.ShapeDtypeStruct((TSHIFT, 2 * bins), BF16),
            jax.ShapeDtypeStruct((2 * detectors, bins, draws), F32),
            jax.ShapeDtypeStruct((detectors, bins, draws), F32),
            jax.ShapeDtypeStruct((16, draws), F32),
        ),
        widths, log_amps, delays, phases.reshape(1, whole), chirps.reshape(1, whole),
        proposal_log.reshape(1, whole), flops=1 << 28, name="terms",
    )
    added = jnp.sum(everyone, axis=0, keepdims=True)
    joined = lax.all_gather(added, "bin", axis=0, tiled=True)
    marginal, stat = call(
        score_kernel,
        (
            jax.ShapeDtypeStruct((1, draws), F32),
            jax.ShapeDtypeStruct((shards * cores, 1, LANES), F32),
        ),
        joined, high, low, features, spread, flat, flops=1 << 30, name="score",
    )
    stats = lax.all_to_all(stat, ("draw", "bin"), 0, 0, tiled=True)
    marginals = lax.all_gather(marginal.reshape(1, 1, draws), "bin", axis=0, tiled=True)
    weights, evidence = call(
        lambda *refs: final_kernel(*refs, draws=whole * shards),
        (
            jax.ShapeDtypeStruct((cores, 1, draws), F32),
            jax.ShapeDtypeStruct((1, 1), F32),
        ),
        stats, marginals, name="final",
    )
    return weights.reshape(whole), evidence.reshape(1)


def solution(mesh):
    placed = (
        P("event", None, "draw"),
        P("event", "draw"),
        P("event"),
        P("event", "draw"),
        P("event", "draw"),
        P(("event", "draw")),
        P(("event", "draw")),
        P(("event", "draw")),
    )
    return jax.shard_map(
        body,
        mesh=mesh,
        in_specs=placed,
        out_specs=(P(("event", "draw")), P("event")),
        check_vma=False,
    )
```

time: 165 us -> 99.5 us (0.60)
  matrix products: 26.9 us -> 0 us
  other arithmetic: 25.7 us -> 0.07 us
  blocking collectives: 28.3 us -> 6.97 us
  Pallas kernels: 0 us -> 9.31 us
  between operations: 6.07 us -> 0.69 us
  starting transfers between devices: 33.2 us -> 38.4 us
  waiting for transfers between devices: 38.3 us -> 35.1 us
  local copies, waits for them, and re-layouts: 6.13 us -> 8.39 us
    dot_general x7 -> x0, matrix products: 26.9 us -> none  [the longest x1 20.2 us: body(): cross_terms = jnp.dot(matrix, features, precision=PRECISE)]
    all_to_all x1 -> x0, blocking collectives: 24.4 us -> none  [copy_for_each(): lax.all_to_all(jnp.broadcast_to(array[None], (count, *array.shape)), axis...]
    pallas_call x0 -> x4, Pallas kernels: none -> 9.31 us  [call(): pl.pallas_call(kernel, out_shape=outs, in_specs=[VMEM] * len(args), out_s...]
    cos x1 -> x0, other arithmetic: 8.71 us -> none  [build_table(): cosine = jnp.cos(angles)[:, None]]
    unnamed x16 -> x21, local copies, waits for them, and re-layouts: 0.06 us -> 7.69 us
    mul x7 -> x0, other arithmetic: 7.57 us -> none  [the longest x1 6.77 us: sample_terms(): amplitude * jnp.cos(phase_low)]
    all_to_all x1 -> x2, starting transfers between devices: 33.2 us -> 38.4 us  [the longest x1 33.2 us: body(): everyone = lax.all_to_all(sums, 'draw', 0, 0, tiled=True)]
    slice x21 -> x0, local copies, waits for them, and re-layouts: 3.32 us -> none  [the longest x18 2.74 us: joined_by_halves(): part[side::2]]
  transfers between devices with their start and end apart: 1 -> 2, of which waited for: 1 -> 2; matrix products, arithmetic and copies ran while one was open for 6% -> 0% of each run, Pallas kernels for 0% -> 4%
where the time goes in v1:
time: 99.5 us; the launch traced here: 98.9 us
  starting transfers between devices  38.4 us (39%)
  waiting for transfers between devices  35.1 us (35%)
  Pallas kernels  9.31 us (9%)
  local copies, waits for them, and re-layouts  8.39 us (8%)
  blocking collectives  6.97 us (7%)
    all_to_all x1, starting transfers between devices, body(): everyone = lax.all_to_all(sums, 'draw', 0, 0, tiled=True)  33.2 us
    all_to_all x1, waiting for transfers between devices, body(): stats = lax.all_to_all(stat, ('draw', 'bin'), 0, 0, tiled=True)  19.1 us
    all_to_all x1, waiting for transfers between devices, body(): everyone = lax.all_to_all(sums, 'draw', 0, 0, tiled=True)  16 us
    pallas_call x4, Pallas kernels, call(): pl.pallas_call(kernel, out_shape=outs, in_specs=[VMEM] * len(args), out_s...  9.31 us
    unnamed x21, local copies, waits for them, and re-layouts  7.69 us
    all_to_all x1, starting transfers between devices, body(): stats = lax.all_to_all(stat, ('draw', 'bin'), 0, 0, tiled=True)  5.23 us
    all_gather x1, blocking collectives, body(): joined = lax.all_gather(added, 'bin', axis=0, tiled=True)  3.88 us
    all_gather x1, blocking collectives, body(): lax.all_gather(marginal.reshape(1, 1, draws), 'bin', axis=0, tiled=True)  3.09 us
  transfers between devices with their start and end apart: 2, of which 2 were waited for; matrix products, arithmetic and copies ran while one was open for 0% of the time, Pallas kernels for 4%

profile of v1, /device:TPU:37, one launch (start us, length us, event | category | flops | bytes accessed | tf_op | source)
XLA Modules:
  0.0 98.9 jit_solution(12236822358488902098)
XLA Ops:
  0.6 0.7 reshape.30.cross_ref
  1.3 0.0 copy-start.2
  1.3 0.7 copy-done.2
  2.0 0.0 copy-start.3
  2.0 0.7 copy-done.3
  2.7 1.1 %summary.1 = f32[32,1,640]{2,1,0:T(1,128)} custom-call(f32[6,256]{1,0:T(8,128)S(1)} %reshape.30.cross_ref, f32[3,256]{1,0:T(4,128)S(1)} %copy-done.2, s32[1,128]{1,0:T(1,128)S(1)} %bitcast.8), custom_call_target="tpu_custom_call" | custom-call | flops 16777216 | bytes 1048576 | tf_op jit(solution)/shard_map/summary/pallas_call | solution.py:45
  3.8 33.2 %all-to-all-start = ((f32[32,1,640]{2,1,0:T(1,128)}), f32[32,1,640]{2,1,0:T(1,128)S(1)}, u32[]{:S(2)}, u32[]{:S(2)}) async-start(f32[32,1,640]{2,1,0:T(1,128)} %summary.1), calls=%async_computation | async-start | bytes 163840 | tf_op jit(solution)/shard_map/all_to_all | solution.py:229
  37.0 0.0 copy-start.4
  37.0 0.6 copy-done.4
  37.6 0.0 copy-start.5
  37.6 0.7 copy-done.5
  38.3 0.0 copy-start.6
  38.3 0.7 copy-done.6
  39.1 0.0 copy-start.7
  39.1 0.7 copy-done.7
  39.7 0.0 copy-start.8
  39.7 0.7 copy-done.8
  40.4 0.0 copy-start.9
  40.4 0.7 copy-done.9
  41.1 4.2 %terms.1 = (bf16[2048,256]{1,0:T(8,128)(2,1)S(1)}, bf16[2048,256]{1,0:T(8,128)(2,1)S(1)}, f32[6,128,512]{2,1,0:T(8,128)S(1)}, f32[3,128,512]{2,1,0:T(8,128)S(1)}, f32[16,512]{1,0:T(8,128)S(1)}) custom-call(s32[1,128]{1,0:T(1,128)S(1)} %bitcast.9, f32[3,1024]{1,0:T(4,128)S(1)} %copy-done.5, f32[3,1024]{1,0:T(4,128)S(1)} %copy-done.6, f32[1,1024]{1,0:T(1,128)S(1)} %bitcast.10, ...), custom_call_target="tpu_custom_call" | custom-call | flops 268435456 | bytes 1048576 | tf_op jit(solution)/shard_map/terms/pallas_call | solution.py:45
  45.3 0.0 copy-start
  45.3 1.0 copy-done
  46.3 16.0 %all-to-all-done = f32[32,1,640]{2,1,0:T(1,128)S(1)} async-done(((f32[32,1,640]{2,1,0:T(1,128)}), f32[32,1,640]{2,1,0:T(1,128)S(1)}, u32[]{:S(2)}, u32[]{:S(2)}) %all-to-all-start) | async-done | bytes 81952 | tf_op jit(solution)/shard_map/all_to_all | solution.py:229
  62.2 0.1 reduce_sum.9
  62.3 3.9 %all-gather.2.sums_ref = f32[2,1,640]{2,1,0:T(1,128)S(1)} all-gather(f32[1,1,640]{2,1,0:T(1,128)S(1)} %reshape.40), channel_id=2, replica_groups=mesh['event'=4,'draw'=32,'bin'=2] {'bin'}, dimensions={0}, use_global_device_ids=true | all-gather | bytes 7680 | tf_op jit(solution)/shard_map/all_gather | solution.py:243
  66.2 0.0 copy-start.1
  66.2 1.2 %copy-done.1 = bf16[2048,256]{1,0:T(8,128)(2,1)S(1)} copy-done((bf16[2048,256]{1,0:T(8,128)(2,1)S(1)}, bf16[2048,256]{1,0:T(8,128)(2,1)}, u32[]{:S(2)}) %copy-start.1) | copy-done | bytes 1048600
  67.4 3.2 %score.1 = (f32[1,512]{1,0:T(1,128)S(1)}, f32[64,1,128]{2,1,0:T(1,128)}) custom-call(f32[2,1,640]{2,1,0:T(1,128)S(1)} %all-gather.2.sums_ref, bf16[2048,256]{1,0:T(8,128)(2,1)S(1)} %get-tuple-element.11.high_ref, bf16[2048,256]{1,0:T(8,128)(2,1)S(1)} %copy-done.1, f32[6,128,512]{2,1,0:T(8,128)S(1)} %get-tuple-element.13.features_ref, ...), custom_call_target="tpu_custom_call" | custom-call | flops 1073741824 | bytes 1048576 | tf_op jit(solution)/shard_map/score/pallas_call | solution.py:45
  70.6 5.2 %all-to-all-start.1 = ((f32[64,1,128]{2,1,0:T(1,128)}), f32[64,1,128]{2,1,0:T(1,128)S(1)}, u32[]{:S(2)}, u32[]{:S(2)}) async-start(f32[64,1,128]{2,1,0:T(1,128)} %get-tuple-element.16), calls=%async_computation.1 | async-start | bytes 65536 | tf_op jit(solution)/shard_map/all_to_all | solution.py:252
  75.8 3.1 %all-gather.3.refs_1_ = f32[2,1,512]{2,1,0:T(1,128)S(1)} all-gather(f32[1,1,512]{2,1,0:T(1,128)S(1)} %bitcast.7), channel_id=3, replica_groups=mesh['event'=4,'draw'=32,'bin'=2] {'bin'}, dimensions={0}, use_global_device_ids=true | all-gather | bytes 6144 | tf_op jit(solution)/shard_map/all_gather | solution.py:253
  78.9 19.1 %all-to-all-done.1.refs_0_ = f32[64,1,128]{2,1,0:T(1,128)S(1)} async-done(((f32[64,1,128]{2,1,0:T(1,128)}), f32[64,1,128]{2,1,0:T(1,128)S(1)}, u32[]{:S(2)}, u32[]{:S(2)}) %all-to-all-start.1) | async-done | bytes 32800 | tf_op jit(solution)/shard_map/all_to_all | solution.py:252
  98.0 0.9 final.1
  (1 shorter events, 0.0 us)
Async XLA Ops:
  1.3 0.7 copy-start.2
  2.0 0.7 copy-start.3
  3.8 58.5 %all-to-all-start = ((f32[32,1,640]{2,1,0:T(1,128)}), f32[32,1,640]{2,1,0:T(1,128)S(1)}, u32[]{:S(2)}, u32[]{:S(2)}) async-start(f32[32,1,640]{2,1,0:T(1,128)} %summary.1), calls=%async_computation | async-start | bytes 163840 | tf_op jit(solution)/shard_map/all_to_all | solution.py:229
  37.0 0.7 copy-start.4
  37.6 0.7 copy-start.5
  38.3 0.7 copy-start.6
  39.1 0.7 copy-start.7
  39.7 0.7 copy-start.8
  40.4 0.7 copy-start.9
  45.3 1.0 copy-start
  66.2 1.2 %copy-start.1 = (bf16[2048,256]{1,0:T(8,128)(2,1)S(1)}, bf16[2048,256]{1,0:T(8,128)(2,1)}, u32[]{:S(2)}) copy-start(bf16[2048,256]{1,0:T(8,128)(2,1)} %copy-done) | copy-start | bytes 3145732
  70.6 27.4 %all-to-all-start.1 = ((f32[64,1,128]{2,1,0:T(1,128)}), f32[64,1,128]{2,1,0:T(1,128)S(1)}, u32[]{:S(2)}, u32[]{:S(2)}) async-start(f32[64,1,128]{2,1,0:T(1,128)} %get-tuple-element.16), calls=%async_computation.1 | async-start | bytes 65536 | tf_op jit(solution)/shard_map/all_to_all | solution.py:252

commit v2 on v1

v2 whole, which is shorter than its diff:
```python
import functools
import math

import jax
import jax.numpy as jnp
import numpy as np
from jax import lax
from jax.experimental import pallas as pl
from jax.experimental.pallas import tpu as pltpu
from jax.sharding import PartitionSpec as P

TSHIFT = 2048
TIME_STEP = 0.125
CHUNK = 128
TAIL = 16
LANES = 128
DET = 3
CHANNELS = 9
SPAN = 71
ROWS = 5
MEET = 0.75
VMEM = pl.BlockSpec(memory_space=pltpu.VMEM)
F32, BF16 = jnp.float32, jnp.bfloat16


def fit(function, terms):
    nodes = 0.125 * (1.0 + np.cos((np.arange(64) + 0.5) * np.pi / 64))
    basis = np.vander(nodes / 0.25, terms, increasing=True)
    found = np.linalg.lstsq(basis, function(np.sqrt(nodes)), rcond=None)[0]
    return [float(c) for c in found / 0.25 ** np.arange(terms)]


COS = fit(lambda r: np.cos(np.pi * r), 7)
SIN = fit(lambda r: np.sin(np.pi * r) / r, 6)


def horner(coefficients, x):
    total = jnp.full_like(x, coefficients[-1])
    for c in coefficients[-2::-1]:
        total = total * x + c
    return total


def turn(u):
    r = u - jnp.round(u)
    square = r * r
    cosine, sine = horner(COS, square), horner(SIN, square) * r
    twice = sine + sine
    return 1.0 - twice * sine, twice * cosine


def call(kernel, outs, *args, scratch=None, limit=24 << 20, flops=1 << 20, name=None):
    where = VMEM
    if scratch is not None:
        where = pl.BlockSpec(memory_space=pltpu.HBM)
        args = [pltpu.with_memory_space_constraint(a, pltpu.HBM) for a in args]
    return pl.pallas_call(
        kernel,
        out_shape=outs,
        in_specs=[where] * len(args),
        out_specs=jax.tree.map(lambda _: VMEM, outs),
        scratch_shapes=() if scratch is None else scratch,
        compiler_params=pltpu.CompilerParams(vmem_limit_bytes=limit),
        cost_estimate=pl.CostEstimate(flops=flops, bytes_accessed=1 << 20, transcendentals=0),
        name=name,
    )(*args)


def landing(args):
    return [pltpu.VMEM(a.shape, a.dtype) for a in args] + [pltpu.SemaphoreType.DMA((len(args),))]


def fetch(sources, targets, semaphores):
    copies = [
        pltpu.make_async_copy(source, target, semaphores.at[i])
        for i, (source, target) in enumerate(zip(sources, targets))
    ]
    for copy in copies:
        copy.start()
    return copies


def shifted(x, amount):
    for bit in range(LANES.bit_length() - 1):
        x = jnp.where((amount >> bit) & 1 == 1, pltpu.roll(x, 1 << bit, 1), x)
    return x


def edges(widths):
    wide = widths.astype(F32)
    bins = wide.shape[1]
    before = lax.broadcasted_iota(jnp.int32, (bins, bins), 0)
    mine = lax.broadcasted_iota(jnp.int32, (bins, bins), 1)
    ones = jnp.where(before <= mine, 1.0, 0.0).astype(BF16)
    rows = jnp.broadcast_to(wide, (16, bins)).astype(BF16)
    upper = jnp.dot(rows, ones, preferred_element_type=F32)[:1]
    return wide, upper


def split(x):
    high = x.astype(BF16)
    return high, (x - high.astype(F32)).astype(BF16)


def summary_kernel(cross_in, power_in, widths_in, out_ref, cross_ref, power_ref, widths_ref, sems):
    for copy in fetch(
        (widths_in, cross_in, power_in), (widths_ref, cross_ref, power_ref), sems
    ):
        copy.wait()
    fine, bins = power_ref.shape[1], widths_ref.shape[1]
    wide, upper = edges(widths_ref[...])
    lower = upper - wide
    first = (lax.axis_index("draw") * fine).astype(F32)
    at = lax.broadcasted_iota(jnp.int32, (fine, bins), 0).astype(F32) + first
    inside = (at >= lower) & (at < upper)
    up = jnp.where(inside, 2.0 * (at - lower) + 1.0, 0.0)
    down = jnp.where(inside, 2.0 * wide - up, 0.0)
    both_high, both_low = split(up * down)
    weights = jnp.concatenate([up.astype(BF16), down.astype(BF16), both_high, both_low], axis=1)
    data = jnp.concatenate(
        [cross_ref[d] for d in range(DET)] + [power_ref[...], jnp.zeros((7, fine), F32)], axis=0
    )
    high = data.astype(BF16)
    rest = data - high.astype(F32)
    middle, low = split(rest)
    got = jnp.dot(
        jnp.concatenate([high, middle, low], axis=0), weights, preferred_element_type=F32
    )
    got = got[:16] + got[16:32] + got[32:]
    scale = 0.5 / wide
    end = got[:, :bins] * scale
    start = got[:, bins : 2 * bins] * scale
    mixed = (got[:, 2 * bins : 3 * bins] + got[:, 3 * bins :]) * (scale * scale)
    row = lax.broadcasted_iota(jnp.int32, (16, bins), 0)
    lane = lax.broadcasted_iota(jnp.int32, (16, bins), 1)
    merged = end + pltpu.roll(start, bins - 1, 1)
    passed = jnp.sum(jnp.where(upper <= first, 1, 0), axis=1, keepdims=True)
    table = shifted(jnp.where(row < 6, merged, mixed), (bins + 1 - passed) % bins)
    total = jnp.sum(data, axis=1, keepdims=True)
    table = jnp.where((row >= 6) & (lane == SPAN - 1), total, table)
    lane = lane[:1]
    tiles = [jnp.zeros((1, bins), F32)] * (ROWS + 1)
    for c in range(CHANNELS):
        tile, off = divmod(c * SPAN, bins)
        line = pltpu.roll(table[c : c + 1], off, 1) if off else table[c : c + 1]
        tiles[tile] = tiles[tile] + jnp.where(lane >= off, line, 0.0)
        tiles[tile + 1] = tiles[tile + 1] + jnp.where(lane < off, line, 0.0)
    for r in range(ROWS):
        out_ref[:, :, r * bins : (r + 1) * bins] = jnp.broadcast_to(
            tiles[r][None], (out_ref.shape[0], 1, bins)
        )


def terms_kernel(
    widths_in, amps_in, delays_in, phases_in, chirps_in, prior_in,
    cos_ref, sin_ref, features_ref, spread_ref, flat_ref, place_ref,
    widths_ref, amps_ref, delays_ref, phases_ref, chirps_ref, prior_ref, sems,
    grid=0.0, fine=0, start=0,
):
    copies = fetch(
        (widths_in, amps_in, delays_in, phases_in, chirps_in, prior_in),
        (widths_ref, amps_ref, delays_ref, phases_ref, chirps_ref, prior_ref),
        sems,
    )
    copies[0].wait()
    wide, upper = edges(widths_ref[...])
    bins = wide.shape[1]
    draws = features_ref.shape[2]
    mine = pl.ds(pl.multiple_of(lax.axis_index("bin") * draws, draws), draws)
    member = lax.broadcasted_iota(jnp.int32, place_ref.shape, 0)
    source = (member + start) % place_ref.shape[0] * fine
    passed = jnp.sum(jnp.where(upper <= source.astype(F32), 1, 0), axis=1, keepdims=True)
    place_ref[...] = jnp.broadcast_to((passed + (bins - 1)) % bins, place_ref.shape)
    step = upper * (TIME_STEP / grid)
    near = lax.broadcasted_iota(jnp.int32, (CHUNK, bins), 0).astype(F32)
    near_cos, near_sin = turn(near * step)
    for first in range(0, TSHIFT // 2 + TAIL, CHUNK):
        size = min(CHUNK, TSHIFT // 2 + TAIL - first)
        rows = slice(first, first + size)
        far_cos, far_sin = turn(float(first) * step)
        here_cos, here_sin = near_cos[:size], near_sin[:size]
        cosine = here_cos * far_cos - here_sin * far_sin
        sine = here_sin * far_cos + here_cos * far_sin
        cos_ref[rows, :bins], cos_ref[rows, bins:] = split(cosine)
        sin_ref[rows, :bins], sin_ref[rows, bins:] = split(sine)
    tall = jnp.concatenate([wide, upper, jnp.zeros((bins - 2, bins), F32)], axis=0).T
    width, x = tall[:, :1] * (1.0 / grid), tall[:, 1:2] * (1.0 / grid)
    for copy in copies[1:]:
        copy.wait()
    chirps = chirps_ref[:, mine]
    base = phases_ref[:, mine] * (0.5 / math.pi)
    common = base + (chirps * (0.5 / math.pi)) * (x * x)
    half_bend = (0.5 * width * (x + (x - width))) * chirps
    cos0, sin0 = turn(base)
    for d in range(DET):
        amp = jnp.exp(amps_ref[d : d + 1, mine])
        delay = delays_ref[d : d + 1, mine]
        cosine, sine = turn(x * delay + common)
        features_ref[2 * d] = amp * cosine
        features_ref[2 * d + 1] = amp * sine
        half = (math.pi * width) * delay + half_bend
        h2 = half * half
        sh = half * (1.0 + h2 * (-1.0 / 6 + h2 * (1.0 / 120 + h2 * (-1.0 / 5040))))
        spread_ref[d] = (2.0 * amp * sh) * (amp * sh)
        flat_ref[2 * d : 2 * d + 1] = amp * cos0
        flat_ref[2 * d + 1 : 2 * d + 2] = amp * sin0
    flat_ref[6:7] = prior_ref[:, mine]


def score_kernel(
    sums_ref, cos_ref, sin_ref, features_ref, spread_ref, flat_ref, place_ref, out_ref, stat_ref,
    zero=0,
):
    bins = features_ref.shape[1]
    draws = features_ref.shape[2]
    place = place_ref[...]
    row = lax.broadcasted_iota(jnp.int32, place.shape, 0)
    lane = lax.broadcasted_iota(jnp.int32, place.shape, 1)
    tiles = [sums_ref[:, 0, r * bins : (r + 1) * bins] for r in range(ROWS)] + [None]
    lines, single = [], []
    for c in range(CHANNELS):
        tile, off = divmod(c * SPAN, bins)
        line = pltpu.roll(tiles[tile], bins - off, 1) if off else tiles[tile]
        if off + SPAN > bins:
            line = jnp.where(lane < bins - off, line, pltpu.roll(tiles[tile + 1], bins - off, 1))
        if c >= 6:
            at_end = jnp.sum(line, axis=0, keepdims=True)[:, SPAN - 1 : SPAN]
        line = shifted(jnp.where(lane < SPAN - (1 if c >= 6 else 0), line, 0.0), place)
        if c < 6:
            at_end = line[zero : zero + 1, bins - 1 :]
            line = jnp.where((row == zero) & (lane == bins - 1), 0.0, line)
        single.append(at_end)
        lines.append(jnp.sum(line, axis=0, keepdims=True))
    tall = jnp.concatenate(lines + [jnp.zeros((bins - CHANNELS, bins), F32)], axis=0).T
    real = imag = power = None
    offset = flat_ref[6:7]
    for d in range(DET):
        a, b, mixed = tall[:, 2 * d : 2 * d + 1], tall[:, 2 * d + 1 : 2 * d + 2], tall[:, 6 + d : 7 + d]
        cosine, sine = features_ref[2 * d], features_ref[2 * d + 1]
        re, im, pw = a * cosine + b * sine, b * cosine - a * sine, mixed * spread_ref[d]
        real = re if real is None else real + re
        imag = im if imag is None else imag + im
        power = pw if power is None else power + pw
        cos0, sin0 = flat_ref[2 * d : 2 * d + 1], flat_ref[2 * d + 1 : 2 * d + 2]
        offset = offset + single[2 * d] * cos0 + single[2 * d + 1] * sin0
        offset = offset - (0.5 * single[6 + d]) * (cos0 * cos0 + sin0 * sin0)
    offset = offset + jnp.sum(power, axis=0, keepdims=True)
    real, imag = (
        [jnp.concatenate([half, half], axis=0) for half in split(part)] for part in (real, imag)
    )

    def rotated(rows):
        return (
            jnp.dot(ref[rows, :], part[0], preferred_element_type=F32)
            + jnp.dot(ref[rows, :], part[1], preferred_element_type=F32)
            for ref, part in ((cos_ref, real), (sin_ref, imag))
        )

    even, odd = rotated(slice(TSHIFT // 2, TSHIFT // 2 + TAIL))
    earliest = (even - odd)[:1]
    top = total = None
    for first in range(0, TSHIFT // 2, CHUNK):
        even, odd = rotated(slice(first, first + CHUNK))
        after, before = even + odd, even - odd
        if first == 0:
            at = lax.broadcasted_iota(jnp.int32, before.shape, 0)
            before = jnp.where(at == 0, earliest, before)
        after = after.reshape(CHUNK // 8, 8, draws)
        before = before.reshape(CHUNK // 8, 8, draws)
        peak = jnp.max(jnp.maximum(after, before), axis=0)
        if top is not None:
            peak = jnp.maximum(peak, top)
            total = total * jnp.exp(top - peak)
        add = jnp.sum(jnp.exp(after - peak[None]) + jnp.exp(before - peak[None]), axis=0)
        total = add if total is None else total + add
        top = peak
    peak = jnp.max(top, axis=0, keepdims=True)
    total = jnp.sum(total * jnp.exp(top - peak), axis=0, keepdims=True)
    marginal = (peak + jnp.log(total) - math.log(TSHIFT)) + offset
    out_ref[...] = marginal
    best = jnp.max(marginal, axis=1, keepdims=True)
    mass = jnp.sum(jnp.exp(marginal - best), axis=1, keepdims=True)
    lane = lax.broadcasted_iota(jnp.int32, (1, LANES), 1)
    stat = jnp.where(lane == 0, best, mass)
    stat_ref[...] = jnp.broadcast_to(stat[None], stat_ref.shape)


def final_kernel(stats_ref, marginal_ref, out_ref, evidence_ref, draws=0):
    stats = stats_ref[...]
    best, mass = stats[:, :, :1], stats[:, :, 1:2]
    top = jnp.max(best, axis=0, keepdims=True)
    total = top + jnp.log(jnp.sum(mass * jnp.exp(best - top), axis=0, keepdims=True))
    out_ref[...] = marginal_ref[...] - total
    evidence_ref[...] = total[0] - math.log(draws)


def body(fine_cross, fine_power, bin_widths, log_amps, delays, phases, chirps, proposal_log):
    shards, cores = lax.axis_size("draw"), lax.axis_size("bin")
    detectors, fine = fine_power.shape
    bins = bin_widths.shape[0]
    whole = log_amps.shape[1]
    draws = whole // cores
    widths = bin_widths.reshape(1, bins)
    turned = [(i + int(shards * MEET)) % shards for i in range(shards)]
    args = (fine_cross, fine_power, widths)
    sums = call(
        summary_kernel,
        jax.ShapeDtypeStruct((shards, 1, ROWS * bins), F32),
        *args, scratch=landing(args), flops=1 << 24, name="summary",
    )
    everyone = lax.all_to_all(sums, "draw", 0, 0, axis_index_groups=[turned], tiled=True)
    args = (
        widths, log_amps, delays, phases.reshape(1, whole), chirps.reshape(1, whole),
        proposal_log.reshape(1, whole),
    )
    terms = call(
        functools.partial(terms_kernel, grid=float(fine * shards), fine=fine, start=turned[0]),
        (
            jax.ShapeDtypeStruct((TSHIFT // 2 + TAIL, 2 * bins), BF16),
            jax.ShapeDtypeStruct((TSHIFT // 2 + TAIL, 2 * bins), BF16),
            jax.ShapeDtypeStruct((2 * detectors, bins, draws), F32),
            jax.ShapeDtypeStruct((detectors, bins, draws), F32),
            jax.ShapeDtypeStruct((8, draws), F32),
            jax.ShapeDtypeStruct((shards, bins), jnp.int32),
        ),
        *args, scratch=landing(args), flops=1 << 28, name="terms",
    )
    marginal, stat = call(
        functools.partial(score_kernel, zero=turned.index(0)),
        (
            jax.ShapeDtypeStruct((1, draws), F32),
            jax.ShapeDtypeStruct((shards * cores, 1, LANES), F32),
        ),
        everyone, *terms, flops=1 << 30, name="score",
    )
    both = [i * cores + c for i in turned for c in range(cores)]
    stats = lax.all_to_all(
        stat, ("draw", "bin"), 0, 0, axis_index_groups=[both], tiled=True
    )
    marginals = lax.all_gather(marginal.reshape(1, 1, draws), "bin", axis=0, tiled=True)
    weights, evidence = call(
        lambda *refs: final_kernel(*refs, draws=whole * shards),
        (
            jax.ShapeDtypeStruct((cores, 1, draws), F32),
            jax.ShapeDtypeStruct((1, 1), F32),
        ),
        stats, marginals, name="final",
    )
    return weights.reshape(whole), evidence.reshape(1)


def solution(mesh):
    placed = (
        P("event", None, "draw"),
        P("event", "draw"),
        P("event"),
        P("event", "draw"),
        P("event", "draw"),
        P(("event", "draw")),
        P(("event", "draw")),
        P(("event", "draw")),
    )
    return jax.shard_map(
        body,
        mesh=mesh,
        in_specs=placed,
        out_specs=(P(("event", "draw")), P("event")),
        check_vma=False,
    )
```

time: 99.5 us -> 86.9 us (0.87)
  starting transfers between devices: 38.4 us -> 51.2 us
  waiting for transfers between devices: 35.1 us -> 23.4 us
  local copies, waits for them, and re-layouts: 8.39 us -> 0 us
  blocking collectives: 6.97 us -> 1.92 us
    all_to_all x2, starting transfers between devices: 38.4 us -> 51.2 us  [the longest x1 33 us: body(): lax.all_to_all(sums, 'draw', 0, 0, axis_index_groups=[turned], tiled=True)]
    all_to_all x2, waiting for transfers between devices: 35.1 us -> 23.4 us  [the longest x1 12.4 us: body(): lax.all_to_all(sums, 'draw', 0, 0, axis_index_groups=[turned], tiled=True)]
    unnamed x21 -> x0, local copies, waits for them, and re-layouts: 7.69 us -> none
    all_gather x1 -> x0, blocking collectives: 3.88 us -> none  [body(): joined = lax.all_gather(added, 'bin', axis=0, tiled=True)]
    all_gather x1, blocking collectives: 3.09 us -> 1.92 us  [body(): lax.all_gather(marginal.reshape(1, 1, draws), 'bin', axis=0, tiled=True)]
  transfers between devices with their start and end apart: 2 -> 2, of which waited for: 2 -> 2; matrix products, arithmetic and copies ran while one was open for 0% -> 0% of each run, Pallas kernels for 4% -> 3%
where the time goes in v2:
time: 86.9 us; the launch traced here: 86.6 us
  starting transfers between devices  51.2 us (59%)
  waiting for transfers between devices  23.4 us (27%)
  Pallas kernels  9.44 us (11%)
  blocking collectives  1.92 us (2%)
    all_to_all x1, starting transfers between devices, body(): lax.all_to_all(sums, 'draw', 0, 0, axis_index_groups=[turned], tiled=True)  33 us
    all_to_all x1, starting transfers between devices, body(): lax.all_to_all(stat, ('draw', 'bin'), 0, 0, axis_index_groups=[both], til...  18.2 us
    all_to_all x1, waiting for transfers between devices, body(): lax.all_to_all(sums, 'draw', 0, 0, axis_index_groups=[turned], tiled=True)  12.4 us
    all_to_all x1, waiting for transfers between devices, body(): lax.all_to_all(stat, ('draw', 'bin'), 0, 0, axis_index_groups=[both], til...  11 us
    pallas_call x4, Pallas kernels, call(): pl.pallas_call(kernel, out_shape=outs, in_specs=[where] * len(args), out_...  9.44 us
    all_gather x1, blocking collectives, body(): lax.all_gather(marginal.reshape(1, 1, draws), 'bin', axis=0, tiled=True)  1.92 us
  transfers between devices with their start and end apart: 2, of which 2 were waited for; matrix products, arithmetic and copies ran while one was open for 0% of the time, Pallas kernels for 3%

profile of v2, /device:TPU:37, one launch (start us, length us, event | category | flops | bytes accessed | tf_op | source)
XLA Modules:
  0.0 86.6 jit_solution(16341915691354575412)
XLA Ops:
  0.6 2.4 %summary.1 = f32[32,1,640]{2,1,0:T(1,128)} custom-call(f32[3,2,256]{2,1,0:T(2,128)} %cross_in.1, f32[3,256]{1,0:T(4,128)} %power_in.1, s32[1,128]{1,0:T(1,128)} %bitcast.8), custom_call_target="tpu_custom_call" | custom-call | flops 16777216 | bytes 1048576 | tf_op jit(solution)/shard_map/summary/pallas_call | solution.py:57
  3.0 33.0 %all-to-all-start = ((f32[32,1,640]{2,1,0:T(1,128)}), f32[32,1,640]{2,1,0:T(1,128)S(1)}, u32[]{:S(2)}, u32[]{:S(2)}) async-start(f32[32,1,640]{2,1,0:T(1,128)} %summary.1), calls=%async_computation | async-start | bytes 163840 | tf_op jit(solution)/shard_map/all_to_all | solution.py:311
  36.0 2.7 %terms.1 = (bf16[1040,256]{1,0:T(8,128)(2,1)S(1)}, bf16[1040,256]{1,0:T(8,128)(2,1)S(1)}, f32[6,128,512]{2,1,0:T(8,128)S(1)}, f32[3,128,512]{2,1,0:T(8,128)S(1)}...) custom-call(s32[1,128]{1,0:T(1,128)} %bitcast.9, f32[3,1024]{1,0:T(4,128)} %amps_in.1, f32[3,1024]{1,0:T(4,128)} %delays_in.1, ...), custom_call_target="tpu_custom_call" | custom-call | flops 268435456 | bytes 1048576 | tf_op jit(solution)/shard_map/terms/pallas_call | solution.py:57
  38.7 12.4 %all-to-all-done.sums_ref = f32[32,1,640]{2,1,0:T(1,128)S(1)} async-done(((f32[32,1,640]{2,1,0:T(1,128)}), f32[32,1,640]{2,1,0:T(1,128)S(1)}, u32[]{:S(2)}, u32[]{:S(2)}) %all-to-all-start) | async-done | bytes 81952 | tf_op jit(solution)/shard_map/all_to_all | solution.py:311
  51.2 3.5 %score.1 = (f32[1,512]{1,0:T(1,128)S(1)}, f32[64,1,128]{2,1,0:T(1,128)}) custom-call(f32[32,1,640]{2,1,0:T(1,128)S(1)} %all-to-all-done.sums_ref, bf16[1040,256]{1,0:T(8,128)(2,1)S(1)} %get-tuple-element.12.cos_ref, bf16[1040,256]{1,0:T(8,128)(2,1)S(1)} %get-tuple-element.13.sin_ref, f32[6,128,512]{2,1,0:T(8,128)S(1)} %get-tuple-element.14.features_ref, ...), custom_call_target="tpu_custom_call" | custom-call | flops 1073741824 | bytes 1048576 | tf_op jit(solution)/shard_map/score/pallas_call | solution.py:57
  54.7 18.2 %all-to-all-start.1 = ((f32[64,1,128]{2,1,0:T(1,128)}), f32[64,1,128]{2,1,0:T(1,128)S(1)}, u32[]{:S(2)}, u32[]{:S(2)}) async-start(f32[64,1,128]{2,1,0:T(1,128)} %get-tuple-element.18), calls=%async_computation.1 | async-start | bytes 65536 | tf_op jit(solution)/shard_map/all_to_all | solution.py:337
  72.9 1.9 %all-gather.1.refs_1_ = f32[2,1,512]{2,1,0:T(1,128)S(1)} all-gather(f32[1,1,512]{2,1,0:T(1,128)S(1)} %bitcast.7), channel_id=2, replica_groups=mesh['event'=4,'draw'=32,'bin'=2] {'bin'}, dimensions={0}, use_global_device_ids=true | all-gather | bytes 6144 | tf_op jit(solution)/shard_map/all_gather | solution.py:340
  74.8 11.0 %all-to-all-done.1.refs_0_ = f32[64,1,128]{2,1,0:T(1,128)S(1)} async-done(((f32[64,1,128]{2,1,0:T(1,128)}), f32[64,1,128]{2,1,0:T(1,128)S(1)}, u32[]{:S(2)}, u32[]{:S(2)}) %all-to-all-start.1) | async-done | bytes 32800 | tf_op jit(solution)/shard_map/all_to_all | solution.py:337
  85.7 0.9 %final.1 = (f32[2,1,512]{2,1,0:T(1,128)}, f32[1,1]{1,0:T(1,128)}) custom-call(f32[64,1,128]{2,1,0:T(1,128)S(1)} %all-to-all-done.1.refs_0_, f32[2,1,512]{2,1,0:T(1,128)S(1)} %all-gather.1.refs_1_), custom_call_target="tpu_custom_call" | custom-call | flops 1048576 | bytes 1048576 | tf_op jit(solution)/shard_map/final/pallas_call | solution.py:57
Async XLA Ops:
  3.0 48.2 %all-to-all-start = ((f32[32,1,640]{2,1,0:T(1,128)}), f32[32,1,640]{2,1,0:T(1,128)S(1)}, u32[]{:S(2)}, u32[]{:S(2)}) async-start(f32[32,1,640]{2,1,0:T(1,128)} %summary.1), calls=%async_computation | async-start | bytes 163840 | tf_op jit(solution)/shard_map/all_to_all | solution.py:311
  54.7 31.1 %all-to-all-start.1 = ((f32[64,1,128]{2,1,0:T(1,128)}), f32[64,1,128]{2,1,0:T(1,128)S(1)}, u32[]{:S(2)}, u32[]{:S(2)}) async-start(f32[64,1,128]{2,1,0:T(1,128)} %get-tuple-element.18), calls=%async_computation.1 | async-start | bytes 65536 | tf_op jit(solution)/shard_map/all_to_all | solution.py:337

commit v3 on v2

--- a/solution.py
+++ b/solution.py
@@ -11,13 +11,17 @@
 
 TSHIFT = 2048
 TIME_STEP = 0.125
+LOG2 = math.log(2.0)
+WIDE = 256
 CHUNK = 128
 TAIL = 16
+STRIP = 128
 LANES = 128
 DET = 3
-CHANNELS = 9
-SPAN = 71
-ROWS = 5
+CHANNELS = 6
+SPAN = 68
+TERMS = 16
+PAYLOAD = CHANNELS * SPAN + DET * TERMS
 MEET = 0.75
 VMEM = pl.BlockSpec(memory_space=pltpu.VMEM)
 F32, BF16 = jnp.float32, jnp.bfloat16
@@ -49,9 +53,9 @@
     return 1.0 - twice * sine, twice * cosine
 
 
-def call(kernel, outs, *args, scratch=None, limit=24 << 20, flops=1 << 20, name=None):
+def call(kernel, outs, *args, scratch=(), pinned=False, limit=24 << 20, flops=1 << 20, name=None):
     where = VMEM
-    if scratch is not None:
+    if pinned:
         where = pl.BlockSpec(memory_space=pltpu.HBM)
         args = [pltpu.with_memory_space_constraint(a, pltpu.HBM) for a in args]
     return pl.pallas_call(
@@ -59,7 +63,7 @@
         out_shape=outs,
         in_specs=[where] * len(args),
         out_specs=jax.tree.map(lambda _: VMEM, outs),
-        scratch_shapes=() if scratch is None else scratch,
+        scratch_shapes=scratch,
         compiler_params=pltpu.CompilerParams(vmem_limit_bytes=limit),
         cost_estimate=pl.CostEstimate(flops=flops, bytes_accessed=1 << 20, transcendentals=0),
         name=name,
@@ -84,6 +88,27 @@
     for bit in range(LANES.bit_length() - 1):
         x = jnp.where((amount >> bit) & 1 == 1, pltpu.roll(x, 1 << bit, 1), x)
     return x
+
+
+def series():
+    return [
+        (-4.0 * c * math.comb(n, j), n - j, j)
+        for n, c in ((2, 1.0), (4, -1.0 / 3), (6, 2.0 / 45))
+        for j in range(n + 1)
+    ]
+
+
+def powers(x, count):
+    found = [None, x]
+    while len(found) <= count:
+        found.append(found[-1] * x)
+    return found
+
+
+def monomial(left, right, i, j):
+    if i and j:
+        return left[i] * right[j]
+    return left[i] if i else right[j]
 
 
 def edges(widths):
@@ -102,7 +127,9 @@
     return high, (x - high.astype(F32)).astype(BF16)
 
 
-def summary_kernel(cross_in, power_in, widths_in, out_ref, cross_ref, power_ref, widths_ref, sems):
+def summary_kernel(
+    cross_in, power_in, widths_in, out_ref, cross_ref, power_ref, widths_ref, sems, grid=0.0
+):
     for copy in fetch(
         (widths_in, cross_in, power_in), (widths_ref, cross_ref, power_ref), sems
     ):
@@ -135,25 +162,37 @@
     lane = lax.broadcasted_iota(jnp.int32, (16, bins), 1)
     merged = end + pltpu.roll(start, bins - 1, 1)
     passed = jnp.sum(jnp.where(upper <= first, 1, 0), axis=1, keepdims=True)
-    table = shifted(jnp.where(row < 6, merged, mixed), (bins + 1 - passed) % bins)
+    table = shifted(merged, (bins + 1 - passed) % bins)
+    width, x = wide * (1.0 / grid), upper * (1.0 / grid)
+    slope = powers(math.pi * width, 6)
+    bend = powers(0.5 * width * (x + (x - width)), 6)
+    factors = [c * monomial(slope, bend, i, j) for c, i, j in series()]
+    factors = jnp.concatenate(factors + [jnp.zeros((1, bins), F32)], axis=0)
+    extra = jnp.zeros((TERMS, bins), F32)
     total = jnp.sum(data, axis=1, keepdims=True)
-    table = jnp.where((row >= 6) & (lane == SPAN - 1), total, table)
+    for d in range(DET):
+        each = jnp.sum(factors * mixed[6 + d : 7 + d], axis=1, keepdims=True)
+        each = jnp.where(row[:, :1] == TERMS - 1, total[6 + d : 7 + d], each)
+        extra = jnp.where(lane == row + (CHANNELS * SPAN % bins + d * TERMS), each, extra)
+    tiles = [jnp.zeros((1, bins), F32)] * 4
+    tiles[3] = jnp.sum(extra, axis=0, keepdims=True)
     lane = lane[:1]
-    tiles = [jnp.zeros((1, bins), F32)] * (ROWS + 1)
     for c in range(CHANNELS):
         tile, off = divmod(c * SPAN, bins)
         line = pltpu.roll(table[c : c + 1], off, 1) if off else table[c : c + 1]
         tiles[tile] = tiles[tile] + jnp.where(lane >= off, line, 0.0)
-        tiles[tile + 1] = tiles[tile + 1] + jnp.where(lane < off, line, 0.0)
-    for r in range(ROWS):
-        out_ref[:, :, r * bins : (r + 1) * bins] = jnp.broadcast_to(
-            tiles[r][None], (out_ref.shape[0], 1, bins)
+        if off + SPAN > bins:
+            tiles[tile + 1] = tiles[tile + 1] + jnp.where(lane < off, line, 0.0)
+    for r, tile in enumerate(tiles):
+        end = min((r + 1) * bins, PAYLOAD)
+        out_ref[:, :, r * bins : end] = jnp.broadcast_to(
+            tile[None, :, : end - r * bins], (out_ref.shape[0], 1, end - r * bins)
         )
 
 
 def terms_kernel(
     widths_in, amps_in, delays_in, phases_in, chirps_in, prior_in,
-    cos_ref, sin_ref, features_ref, spread_ref, flat_ref, place_ref,
+    cos_ref, sin_ref, features_ref, flat_ref, place_ref,
     widths_ref, amps_ref, delays_ref, phases_ref, chirps_ref, prior_ref, sems,
     grid=0.0, fine=0, start=0,
 ):
@@ -183,14 +222,13 @@
         sine = here_sin * far_cos + here_cos * far_sin
         cos_ref[rows, :bins], cos_ref[rows, bins:] = split(cosine)
         sin_ref[rows, :bins], sin_ref[rows, bins:] = split(sine)
-    tall = jnp.concatenate([wide, upper, jnp.zeros((bins - 2, bins), F32)], axis=0).T
-    width, x = tall[:, :1] * (1.0 / grid), tall[:, 1:2] * (1.0 / grid)
+    tall = jnp.concatenate([upper, jnp.zeros((bins - 1, bins), F32)], axis=0).T
+    x = tall[:, :1] * (1.0 / grid)
     for copy in copies[1:]:
         copy.wait()
     chirps = chirps_ref[:, mine]
     base = phases_ref[:, mine] * (0.5 / math.pi)
     common = base + (chirps * (0.5 / math.pi)) * (x * x)
-    half_bend = (0.5 * width * (x + (x - width))) * chirps
     cos0, sin0 = turn(base)
     for d in range(DET):
         amp = jnp.exp(amps_ref[d : d + 1, mine])
@@ -198,85 +236,97 @@
         cosine, sine = turn(x * delay + common)
         features_ref[2 * d] = amp * cosine
         features_ref[2 * d + 1] = amp * sine
-        half = (math.pi * width) * delay + half_bend
-        h2 = half * half
-        sh = half * (1.0 + h2 * (-1.0 / 6 + h2 * (1.0 / 120 + h2 * (-1.0 / 5040))))
-        spread_ref[d] = (2.0 * amp * sh) * (amp * sh)
         flat_ref[2 * d : 2 * d + 1] = amp * cos0
         flat_ref[2 * d + 1 : 2 * d + 2] = amp * sin0
     flat_ref[6:7] = prior_ref[:, mine]
+    flat_ref[7:8] = chirps
+    flat_ref[8 : 8 + DET] = delays_ref[:, mine]
+    flat_ref[8 + DET :] = jnp.zeros((8 - DET, draws), F32)
 
 
 def score_kernel(
-    sums_ref, cos_ref, sin_ref, features_ref, spread_ref, flat_ref, place_ref, out_ref, stat_ref,
+    sums_ref, cos_ref, sin_ref, features_ref, flat_ref, place_ref, out_ref, stat_ref,
     zero=0,
 ):
     bins = features_ref.shape[1]
     draws = features_ref.shape[2]
+    half = TSHIFT // 2
     place = place_ref[...]
     row = lax.broadcasted_iota(jnp.int32, place.shape, 0)
     lane = lax.broadcasted_iota(jnp.int32, place.shape, 1)
-    tiles = [sums_ref[:, 0, r * bins : (r + 1) * bins] for r in range(ROWS)] + [None]
+    tiles = [sums_ref[:, 0, r * bins : (r + 1) * bins] for r in range(3)]
+    last = sums_ref[:, 0, 3 * bins : PAYLOAD]
+    rest = jnp.zeros((last.shape[0], 4 * bins - PAYLOAD), F32)
+    tiles.append(jnp.concatenate([last, rest], axis=1))
     lines, single = [], []
     for c in range(CHANNELS):
         tile, off = divmod(c * SPAN, bins)
         line = pltpu.roll(tiles[tile], bins - off, 1) if off else tiles[tile]
         if off + SPAN > bins:
             line = jnp.where(lane < bins - off, line, pltpu.roll(tiles[tile + 1], bins - off, 1))
-        if c >= 6:
-            at_end = jnp.sum(line, axis=0, keepdims=True)[:, SPAN - 1 : SPAN]
-        line = shifted(jnp.where(lane < SPAN - (1 if c >= 6 else 0), line, 0.0), place)
-        if c < 6:
-            at_end = line[zero : zero + 1, bins - 1 :]
-            line = jnp.where((row == zero) & (lane == bins - 1), 0.0, line)
-        single.append(at_end)
+        line = shifted(jnp.where(lane < SPAN, line, 0.0), place)
+        single.append(line[zero : zero + 1, bins - 1 :])
+        line = jnp.where((row == zero) & (lane == bins - 1), 0.0, line)
         lines.append(jnp.sum(line, axis=0, keepdims=True))
     tall = jnp.concatenate(lines + [jnp.zeros((bins - CHANNELS, bins), F32)], axis=0).T
-    real = imag = power = None
+    extra = jnp.sum(tiles[3], axis=0, keepdims=True)
+    extra = [
+        pltpu.roll(extra, bins - CHANNELS * SPAN % bins - d * TERMS, 1) for d in range(DET)
+    ]
+    extra = jnp.concatenate(extra + [jnp.zeros((8 - DET, bins), F32)], axis=0)
+    chirp = powers(jnp.broadcast_to(flat_ref[7:8], (8, draws)), 6)
+    delay = powers(flat_ref[8:], 6)
+    power = jnp.broadcast_to(extra[:, TERMS - 1 : TERMS], (8, draws))
+    for k, (_, i, j) in enumerate(series()):
+        power = power + extra[:, k : k + 1] * monomial(delay, chirp, i, j)
+    real = imag = None
     offset = flat_ref[6:7]
     for d in range(DET):
-        a, b, mixed = tall[:, 2 * d : 2 * d + 1], tall[:, 2 * d + 1 : 2 * d + 2], tall[:, 6 + d : 7 + d]
+        a, b = tall[:, 2 * d : 2 * d + 1], tall[:, 2 * d + 1 : 2 * d + 2]
         cosine, sine = features_ref[2 * d], features_ref[2 * d + 1]
-        re, im, pw = a * cosine + b * sine, b * cosine - a * sine, mixed * spread_ref[d]
+        re, im = a * cosine + b * sine, b * cosine - a * sine
         real = re if real is None else real + re
         imag = im if imag is None else imag + im
-        power = pw if power is None else power + pw
         cos0, sin0 = flat_ref[2 * d : 2 * d + 1], flat_ref[2 * d + 1 : 2 * d + 2]
         offset = offset + single[2 * d] * cos0 + single[2 * d + 1] * sin0
-        offset = offset - (0.5 * single[6 + d]) * (cos0 * cos0 + sin0 * sin0)
-    offset = offset + jnp.sum(power, axis=0, keepdims=True)
+        offset = offset - (0.5 * power[d : d + 1]) * (cos0 * cos0 + sin0 * sin0)
     real, imag = (
-        [jnp.concatenate([half, half], axis=0) for half in split(part)] for part in (real, imag)
-    )
-
-    def rotated(rows):
+        [jnp.concatenate([piece, piece], axis=0) for piece in split(part * (1.0 / LOG2))]
+        for part in (real, imag)
+    )
+
+    def rotated(rows, columns):
         return (
-            jnp.dot(ref[rows, :], part[0], preferred_element_type=F32)
-            + jnp.dot(ref[rows, :], part[1], preferred_element_type=F32)
+            jnp.dot(ref[rows, :], part[0][:, columns], preferred_element_type=F32)
+            + jnp.dot(ref[rows, :], part[1][:, columns], preferred_element_type=F32)
             for ref, part in ((cos_ref, real), (sin_ref, imag))
         )
 
-    even, odd = rotated(slice(TSHIFT // 2, TSHIFT // 2 + TAIL))
-    earliest = (even - odd)[:1]
-    top = total = None
-    for first in range(0, TSHIFT // 2, CHUNK):
-        even, odd = rotated(slice(first, first + CHUNK))
-        after, before = even + odd, even - odd
-        if first == 0:
-            at = lax.broadcasted_iota(jnp.int32, before.shape, 0)
-            before = jnp.where(at == 0, earliest, before)
-        after = after.reshape(CHUNK // 8, 8, draws)
-        before = before.reshape(CHUNK // 8, 8, draws)
-        peak = jnp.max(jnp.maximum(after, before), axis=0)
-        if top is not None:
-            peak = jnp.maximum(peak, top)
-            total = total * jnp.exp(top - peak)
-        add = jnp.sum(jnp.exp(after - peak[None]) + jnp.exp(before - peak[None]), axis=0)
-        total = add if total is None else total + add
-        top = peak
-    peak = jnp.max(top, axis=0, keepdims=True)
-    total = jnp.sum(total * jnp.exp(top - peak), axis=0, keepdims=True)
-    marginal = (peak + jnp.log(total) - math.log(TSHIFT)) + offset
+    marginal = []
+    for start in range(0, draws, WIDE):
+        columns = slice(start, start + WIDE)
+        even, odd = rotated(slice(half, half + TAIL), columns)
+        earliest = (even - odd)[:1]
+        top = total = None
+        for first in range(0, half, STRIP):
+            even, odd = rotated(slice(first, first + STRIP), columns)
+            after, before = even + odd, even - odd
+            if first == 0:
+                at = lax.broadcasted_iota(jnp.int32, before.shape, 0)
+                before = jnp.where(at == 0, earliest, before)
+            after = after.reshape(STRIP // 8, 8, WIDE)
+            before = before.reshape(STRIP // 8, 8, WIDE)
+            peak = jnp.max(jnp.maximum(after, before), axis=0)
+            if top is not None:
+                peak = jnp.maximum(peak, top)
+                total = total * jnp.exp2(top - peak)
+            add = jnp.sum(jnp.exp2(after - peak[None]) + jnp.exp2(before - peak[None]), axis=0)
+            total = add if total is None else total + add
+            top = peak
+        peak = jnp.max(top, axis=0, keepdims=True)
+        total = jnp.sum(total * jnp.exp2(top - peak), axis=0, keepdims=True)
+        marginal.append(peak * LOG2 + (jnp.log(total) - math.log(TSHIFT)))
+    marginal = jnp.concatenate(marginal, axis=1) + offset
     out_ref[...] = marginal
     best = jnp.max(marginal, axis=1, keepdims=True)
     mass = jnp.sum(jnp.exp(marginal - best), axis=1, keepdims=True)
@@ -304,9 +354,9 @@
     turned = [(i + int(shards * MEET)) % shards for i in range(shards)]
     args = (fine_cross, fine_power, widths)
     sums = call(
-        summary_kernel,
-        jax.ShapeDtypeStruct((shards, 1, ROWS * bins), F32),
-        *args, scratch=landing(args), flops=1 << 24, name="summary",
+        functools.partial(summary_kernel, grid=float(fine * shards)),
+        jax.ShapeDtypeStruct((shards, 1, PAYLOAD), F32),
+        *args, scratch=landing(args), pinned=True, flops=1 << 24, name="summary",
     )
     everyone = lax.all_to_all(sums, "draw", 0, 0, axis_index_groups=[turned], tiled=True)
     args = (
@@ -319,11 +369,10 @@
             jax.ShapeDtypeStruct((TSHIFT // 2 + TAIL, 2 * bins), BF16),
             jax.ShapeDtypeStruct((TSHIFT // 2 + TAIL, 2 * bins), BF16),
             jax.ShapeDtypeStruct((2 * detectors, bins, draws), F32),
-            jax.ShapeDtypeStruct((detectors, bins, draws), F32),
-            jax.ShapeDtypeStruct((8, draws), F32),
+            jax.ShapeDtypeStruct((16, draws), F32),
             jax.ShapeDtypeStruct((shards, bins), jnp.int32),
         ),
-        *args, scratch=landing(args), flops=1 << 28, name="terms",
+        *args, scratch=landing(args), pinned=True, flops=1 << 28, name="terms",
     )
     marginal, stat = call(
         functools.partial(score_kernel, zero=turned.index(0)),

time: 86.9 us -> 85.4 us (0.983)
  waiting for transfers between devices: 23.4 us -> 22.3 us
    all_to_all x1, waiting for transfers between devices: 12.4 us -> 11.3 us  [body(): lax.all_to_all(sums, 'draw', 0, 0, axis_index_groups=[turned], tiled=True)]
where the time goes in v3:
time: 85.4 us; the launch traced here: 85.1 us
  starting transfers between devices  50.8 us (59%)
  waiting for transfers between devices  22.3 us (26%)
  Pallas kernels  9.4 us (11%)
  blocking collectives  1.92 us (2%)
    all_to_all x1, starting transfers between devices, body(): lax.all_to_all(sums, 'draw', 0, 0, axis_index_groups=[turned], tiled=True)  33 us
    all_to_all x1, starting transfers between devices, body(): lax.all_to_all(stat, ('draw', 'bin'), 0, 0, axis_index_groups=[both], til...  17.7 us
    all_to_all x1, waiting for transfers between devices, body(): lax.all_to_all(sums, 'draw', 0, 0, axis_index_groups=[turned], tiled=True)  11.3 us
    all_to_all x1, waiting for transfers between devices, body(): lax.all_to_all(stat, ('draw', 'bin'), 0, 0, axis_index_groups=[both], til...  11 us
    pallas_call x4, Pallas kernels, call(): pl.pallas_call(kernel, out_shape=outs, in_specs=[where] * len(args), out_...  9.4 us
    all_gather x1, blocking collectives, body(): lax.all_gather(marginal.reshape(1, 1, draws), 'bin', axis=0, tiled=True)  1.92 us
  transfers between devices with their start and end apart: 2, of which 2 were waited for; matrix products, arithmetic and copies ran while one was open for 0% of the time, Pallas kernels for 3%

profile of v3, /device:TPU:37, one launch (start us, length us, event | category | flops | bytes accessed | tf_op | source)
XLA Modules:
  0.0 85.1 jit_solution(17013669418580217745)
XLA Ops:
  0.6 2.3 %summary.1 = f32[32,1,456]{2,1,0:T(1,128)} custom-call(f32[3,2,256]{2,1,0:T(2,128)} %cross_in.1, f32[3,256]{1,0:T(4,128)} %power_in.1, s32[1,128]{1,0:T(1,128)} %bitcast.8), custom_call_target="tpu_custom_call" | custom-call | flops 16777216 | bytes 1048576 | tf_op jit(solution)/shard_map/summary/pallas_call | solution.py:61
  3.0 33.0 %all-to-all-start = ((f32[32,1,456]{2,1,0:T(1,128)}), f32[32,1,456]{2,1,0:T(1,128)S(1)}, u32[]{:S(2)}, u32[]{:S(2)}) async-start(f32[32,1,456]{2,1,0:T(1,128)} %summary.1), calls=%async_computation | async-start | bytes 131072 | tf_op jit(solution)/shard_map/all_to_all | solution.py:361
  36.0 2.8 %terms.1 = (bf16[1040,256]{1,0:T(8,128)(2,1)S(1)}, bf16[1040,256]{1,0:T(8,128)(2,1)S(1)}, f32[6,128,512]{2,1,0:T(8,128)S(1)}, f32[16,512]{1,0:T(8,128)S(1)}, s32[32,128]{1,0:T(8,128)S(1)}) custom-call(s32[1,128]{1,0:T(1,128)} %bitcast.9, f32[3,1024]{1,0:T(4,128)} %amps_in.1, f32[3,1024]{1,0:T(4,128)} %delays_in.1, f32[1,1024]{1,0:T(1,128)} %bitcast.10, ...), custom_call_target="tpu_custom_call" | custom-call | flops 268435456 | bytes 1048576 | tf_op jit(solution)/shard_map/terms/pallas_call | solution.py:61
  38.8 11.3 %all-to-all-done.sums_ref = f32[32,1,456]{2,1,0:T(1,128)S(1)} async-done(((f32[32,1,456]{2,1,0:T(1,128)}), f32[32,1,456]{2,1,0:T(1,128)S(1)}, u32[]{:S(2)}, u32[]{:S(2)}) %all-to-all-start) | async-done | bytes 58400 | tf_op jit(solution)/shard_map/all_to_all | solution.py:361
  50.1 3.4 %score.1 = (f32[1,512]{1,0:T(1,128)S(1)}, f32[64,1,128]{2,1,0:T(1,128)}) custom-call(f32[32,1,456]{2,1,0:T(1,128)S(1)} %all-to-all-done.sums_ref, bf16[1040,256]{1,0:T(8,128)(2,1)S(1)} %get-tuple-element.11.cos_ref, bf16[1040,256]{1,0:T(8,128)(2,1)S(1)} %get-tuple-element.12.sin_ref, f32[6,128,512]{2,1,0:T(8,128)S(1)} %get-tuple-element.13.features_ref, ...), custom_call_target="tpu_custom_call" | custom-call | flops 1073741824 | bytes 1048576 | tf_op jit(solution)/shard_map/score/pallas_call | solution.py:61
  53.5 17.7 %all-to-all-start.1 = ((f32[64,1,128]{2,1,0:T(1,128)}), f32[64,1,128]{2,1,0:T(1,128)S(1)}, u32[]{:S(2)}, u32[]{:S(2)}) async-start(f32[64,1,128]{2,1,0:T(1,128)} %get-tuple-element.16), calls=%async_computation.1 | async-start | bytes 65536 | tf_op jit(solution)/shard_map/all_to_all | solution.py:386
  71.3 1.9 %all-gather.1.refs_1_ = f32[2,1,512]{2,1,0:T(1,128)S(1)} all-gather(f32[1,1,512]{2,1,0:T(1,128)S(1)} %bitcast.7), channel_id=2, replica_groups=mesh['event'=4,'draw'=32,'bin'=2] {'bin'}, dimensions={0}, use_global_device_ids=true | all-gather | bytes 6144 | tf_op jit(solution)/shard_map/all_gather | solution.py:389
  73.2 11.0 %all-to-all-done.1.refs_0_ = f32[64,1,128]{2,1,0:T(1,128)S(1)} async-done(((f32[64,1,128]{2,1,0:T(1,128)}), f32[64,1,128]{2,1,0:T(1,128)S(1)}, u32[]{:S(2)}, u32[]{:S(2)}) %all-to-all-start.1) | async-done | bytes 32800 | tf_op jit(solution)/shard_map/all_to_all | solution.py:386
  84.1 0.9 %final.1 = (f32[2,1,512]{2,1,0:T(1,128)}, f32[1,1]{1,0:T(1,128)}) custom-call(f32[64,1,128]{2,1,0:T(1,128)S(1)} %all-to-all-done.1.refs_0_, f32[2,1,512]{2,1,0:T(1,128)S(1)} %all-gather.1.refs_1_), custom_call_target="tpu_custom_call" | custom-call | flops 1048576 | bytes 1048576 | tf_op jit(solution)/shard_map/final/pallas_call | solution.py:61
Async XLA Ops:
  3.0 47.1 %all-to-all-start = ((f32[32,1,456]{2,1,0:T(1,128)}), f32[32,1,456]{2,1,0:T(1,128)S(1)}, u32[]{:S(2)}, u32[]{:S(2)}) async-start(f32[32,1,456]{2,1,0:T(1,128)} %summary.1), calls=%async_computation | async-start | bytes 131072 | tf_op jit(solution)/shard_map/all_to_all | solution.py:361
  53.5 30.6 %all-to-all-start.1 = ((f32[64,1,128]{2,1,0:T(1,128)}), f32[64,1,128]{2,1,0:T(1,128)S(1)}, u32[]{:S(2)}, u32[]{:S(2)}) async-start(f32[64,1,128]{2,1,0:T(1,128)} %get-tuple-element.16), calls=%async_computation.1 | async-start | bytes 65536 | tf_op jit(solution)/shard_map/all_to_all | solution.py:386

commit v4 on v3

--- a/solution.py
+++ b/solution.py
@@ -335,11 +335,21 @@
     stat_ref[...] = jnp.broadcast_to(stat[None], stat_ref.shape)
 
 
-def final_kernel(stats_ref, marginal_ref, out_ref, evidence_ref, draws=0):
-    stats = stats_ref[...]
+def merged(stats):
     best, mass = stats[:, :, :1], stats[:, :, 1:2]
     top = jnp.max(best, axis=0, keepdims=True)
-    total = top + jnp.log(jnp.sum(mass * jnp.exp(best - top), axis=0, keepdims=True))
+    return top, jnp.sum(mass * jnp.exp(best - top), axis=0, keepdims=True)
+
+
+def half_kernel(stats_ref, out_ref):
+    top, mass = merged(stats_ref[...])
+    lane = lax.broadcasted_iota(jnp.int32, out_ref.shape, 2)
+    out_ref[...] = jnp.where(lane == 0, top, mass)
+
+
+def final_kernel(stats_ref, marginal_ref, out_ref, evidence_ref, draws=0):
+    top, mass = merged(stats_ref[...])
+    total = top + jnp.log(mass)
     out_ref[...] = marginal_ref[...] - total
     evidence_ref[...] = total[0] - math.log(draws)
 
@@ -378,22 +388,21 @@
         functools.partial(score_kernel, zero=turned.index(0)),
         (
             jax.ShapeDtypeStruct((1, draws), F32),
-            jax.ShapeDtypeStruct((shards * cores, 1, LANES), F32),
+            jax.ShapeDtypeStruct((shards, 1, LANES), F32),
         ),
         everyone, *terms, flops=1 << 30, name="score",
     )
-    both = [i * cores + c for i in turned for c in range(cores)]
-    stats = lax.all_to_all(
-        stat, ("draw", "bin"), 0, 0, axis_index_groups=[both], tiled=True
-    )
+    stats = lax.all_to_all(stat, "draw", 0, 0, axis_index_groups=[turned], tiled=True)
     marginals = lax.all_gather(marginal.reshape(1, 1, draws), "bin", axis=0, tiled=True)
+    half = call(half_kernel, jax.ShapeDtypeStruct((1, 1, LANES), F32), stats, name="half")
+    halves = lax.all_gather(half, "bin", axis=0, tiled=True)
     weights, evidence = call(
         lambda *refs: final_kernel(*refs, draws=whole * shards),
         (
             jax.ShapeDtypeStruct((cores, 1, draws), F32),
             jax.ShapeDtypeStruct((1, 1), F32),
         ),
-        stats, marginals, name="final",
+        halves, marginals, name="final",
     )
     return weights.reshape(whole), evidence.reshape(1)
 

time: 85.4 us -> 85.5 us (level)
  blocking collectives: 1.92 us -> 10 us
  waiting for transfers between devices: 22.3 us -> 18.1 us
  starting transfers between devices: 50.8 us -> 46.9 us
    all_gather x0 -> x1, blocking collectives: none -> 5.49 us  [body(): halves = lax.all_gather(half, 'bin', axis=0, tiled=True)]
    all_to_all x1, waiting for transfers between devices: 11 us -> 6.72 us  [body(): lax.all_to_all(stat, 'draw', 0, 0, axis_index_groups=[turned], tiled=True)]
    all_to_all x1, starting transfers between devices: 17.7 us -> 13.9 us  [body(): lax.all_to_all(stat, 'draw', 0, 0, axis_index_groups=[turned], tiled=True)]
    all_gather x1, blocking collectives: 1.92 us -> 4.51 us  [body(): lax.all_gather(marginal.reshape(1, 1, draws), 'bin', axis=0, tiled=True)]
    pallas_call x4 -> x5, Pallas kernels: 9.4 us -> 9.49 us  [call(): pl.pallas_call(kernel, out_shape=outs, in_specs=[where] * len(args), out_...]
where the time goes in v4:
time: 85.5 us; the launch traced here: 85.2 us
  starting transfers between devices  46.9 us (55%)
  waiting for transfers between devices  18.1 us (21%)
  blocking collectives  10 us (12%)
  Pallas kernels  9.49 us (11%)
    all_to_all x1, starting transfers between devices, body(): lax.all_to_all(sums, 'draw', 0, 0, axis_index_groups=[turned], tiled=True)  33 us
    all_to_all x1, starting transfers between devices, body(): lax.all_to_all(stat, 'draw', 0, 0, axis_index_groups=[turned], tiled=True)  13.9 us
    all_to_all x1, waiting for transfers between devices, body(): lax.all_to_all(sums, 'draw', 0, 0, axis_index_groups=[turned], tiled=True)  11.3 us
    pallas_call x5, Pallas kernels, call(): pl.pallas_call(kernel, out_shape=outs, in_specs=[where] * len(args), out_...  9.49 us
    all_to_all x1, waiting for transfers between devices, body(): lax.all_to_all(stat, 'draw', 0, 0, axis_index_groups=[turned], tiled=True)  6.72 us
    all_gather x1, blocking collectives, body(): halves = lax.all_gather(half, 'bin', axis=0, tiled=True)  5.49 us
    all_gather x1, blocking collectives, body(): lax.all_gather(marginal.reshape(1, 1, draws), 'bin', axis=0, tiled=True)  4.51 us
  transfers between devices with their start and end apart: 2, of which 2 were waited for; matrix products, arithmetic and copies ran while one was open for 0% of the time, Pallas kernels for 3%

profile of v4, /device:TPU:37, one launch (start us, length us, event | category | flops | bytes accessed | tf_op | source)
XLA Modules:
  0.0 85.2 jit_solution(4054391064432895916)
XLA Ops:
  0.6 2.3 %summary.1 = f32[32,1,456]{2,1,0:T(1,128)} custom-call(f32[3,2,256]{2,1,0:T(2,128)} %cross_in.1, f32[3,256]{1,0:T(4,128)} %power_in.1, s32[1,128]{1,0:T(1,128)} %bitcast.8), custom_call_target="tpu_custom_call" | custom-call | flops 16777216 | bytes 1048576 | tf_op jit(solution)/shard_map/summary/pallas_call | solution.py:61
  3.0 33.0 %all-to-all-start = ((f32[32,1,456]{2,1,0:T(1,128)}), f32[32,1,456]{2,1,0:T(1,128)S(1)}, u32[]{:S(2)}, u32[]{:S(2)}) async-start(f32[32,1,456]{2,1,0:T(1,128)} %summary.1), calls=%async_computation | async-start | bytes 131072 | tf_op jit(solution)/shard_map/all_to_all | solution.py:371
  36.0 2.8 %terms.1 = (bf16[1040,256]{1,0:T(8,128)(2,1)S(1)}, bf16[1040,256]{1,0:T(8,128)(2,1)S(1)}, f32[6,128,512]{2,1,0:T(8,128)S(1)}, f32[16,512]{1,0:T(8,128)S(1)}, s32[32,128]{1,0:T(8,128)S(1)}) custom-call(s32[1,128]{1,0:T(1,128)} %bitcast.9, f32[3,1024]{1,0:T(4,128)} %amps_in.1, f32[3,1024]{1,0:T(4,128)} %delays_in.1, f32[1,1024]{1,0:T(1,128)} %bitcast.10, ...), custom_call_target="tpu_custom_call" | custom-call | flops 268435456 | bytes 1048576 | tf_op jit(solution)/shard_map/terms/pallas_call | solution.py:61
  38.8 11.3 %all-to-all-done.sums_ref = f32[32,1,456]{2,1,0:T(1,128)S(1)} async-done(((f32[32,1,456]{2,1,0:T(1,128)}), f32[32,1,456]{2,1,0:T(1,128)S(1)}, u32[]{:S(2)}, u32[]{:S(2)}) %all-to-all-start) | async-done | bytes 58400 | tf_op jit(solution)/shard_map/all_to_all | solution.py:371
  50.1 3.4 %score.1 = (f32[1,512]{1,0:T(1,128)S(1)}, f32[32,1,128]{2,1,0:T(1,128)}) custom-call(f32[32,1,456]{2,1,0:T(1,128)S(1)} %all-to-all-done.sums_ref, bf16[1040,256]{1,0:T(8,128)(2,1)S(1)} %get-tuple-element.11.cos_ref, bf16[1040,256]{1,0:T(8,128)(2,1)S(1)} %get-tuple-element.12.sin_ref, f32[6,128,512]{2,1,0:T(8,128)S(1)} %get-tuple-element.13.features_ref, ...), custom_call_target="tpu_custom_call" | custom-call | flops 1073741824 | bytes 1048576 | tf_op jit(solution)/shard_map/score/pallas_call | solution.py:61
  53.5 13.9 %all-to-all-start.1 = ((f32[32,1,128]{2,1,0:T(1,128)}), f32[32,1,128]{2,1,0:T(1,128)S(1)}, u32[]{:S(2)}, u32[]{:S(2)}) async-start(f32[32,1,128]{2,1,0:T(1,128)} %get-tuple-element.16), calls=%async_computation.1 | async-start | bytes 32768 | tf_op jit(solution)/shard_map/all_to_all | solution.py:395
  67.4 4.5 %all-gather.1.refs_1_ = f32[2,1,512]{2,1,0:T(1,128)S(1)} all-gather(f32[1,1,512]{2,1,0:T(1,128)S(1)} %bitcast.7), channel_id=2, replica_groups=mesh['event'=4,'draw'=32,'bin'=2] {'bin'}, dimensions={0}, use_global_device_ids=true | all-gather | bytes 6144 | tf_op jit(solution)/shard_map/all_gather | solution.py:396
  71.9 6.7 %all-to-all-done.1.stats_ref = f32[32,1,128]{2,1,0:T(1,128)S(1)} async-done(((f32[32,1,128]{2,1,0:T(1,128)}), f32[32,1,128]{2,1,0:T(1,128)S(1)}, u32[]{:S(2)}, u32[]{:S(2)}) %all-to-all-start.1) | async-done | bytes 16416 | tf_op jit(solution)/shard_map/all_to_all | solution.py:395
  78.7 0.2 half.1
  78.8 5.5 %all_gather.6.refs_0_ = f32[2,1,128]{2,1,0:T(1,128)S(1)} all-gather(f32[1,1,128]{2,1,0:T(1,128)S(1)} %half.1), channel_id=1, replica_groups=mesh['event'=4,'draw'=32,'bin'=2] {'bin'}, dimensions={0}, use_global_device_ids=true | all-gather | bytes 1536 | tf_op jit(solution)/shard_map/all_gather | solution.py:398
  84.3 0.8 final.1
Async XLA Ops:
  3.0 47.1 %all-to-all-start = ((f32[32,1,456]{2,1,0:T(1,128)}), f32[32,1,456]{2,1,0:T(1,128)S(1)}, u32[]{:S(2)}, u32[]{:S(2)}) async-start(f32[32,1,456]{2,1,0:T(1,128)} %summary.1), calls=%async_computation | async-start | bytes 131072 | tf_op jit(solution)/shard_map/all_to_all | solution.py:371
  53.5 25.1 %all-to-all-start.1 = ((f32[32,1,128]{2,1,0:T(1,128)}), f32[32,1,128]{2,1,0:T(1,128)S(1)}, u32[]{:S(2)}, u32[]{:S(2)}) async-start(f32[32,1,128]{2,1,0:T(1,128)} %get-tuple-element.16), calls=%async_computation.1 | async-start | bytes 32768 | tf_op jit(solution)/shard_map/all_to_all | solution.py:395

commit v5 on v4

--- a/solution.py
+++ b/solution.py
@@ -245,8 +245,7 @@
 
 
 def score_kernel(
-    sums_ref, cos_ref, sin_ref, features_ref, flat_ref, place_ref, out_ref, stat_ref,
-    zero=0,
+    sums_ref, cos_ref, sin_ref, features_ref, flat_ref, place_ref, out_ref, zero=0,
 ):
     bins = features_ref.shape[1]
     draws = features_ref.shape[2]
@@ -327,12 +326,7 @@
         total = jnp.sum(total * jnp.exp2(top - peak), axis=0, keepdims=True)
         marginal.append(peak * LOG2 + (jnp.log(total) - math.log(TSHIFT)))
     marginal = jnp.concatenate(marginal, axis=1) + offset
-    out_ref[...] = marginal
-    best = jnp.max(marginal, axis=1, keepdims=True)
-    mass = jnp.sum(jnp.exp(marginal - best), axis=1, keepdims=True)
-    lane = lax.broadcasted_iota(jnp.int32, (1, LANES), 1)
-    stat = jnp.where(lane == 0, best, mass)
-    stat_ref[...] = jnp.broadcast_to(stat[None], stat_ref.shape)
+    out_ref[...] = marginal[None]
 
 
 def merged(stats):
@@ -341,10 +335,13 @@
     return top, jnp.sum(mass * jnp.exp(best - top), axis=0, keepdims=True)
 
 
-def half_kernel(stats_ref, out_ref):
-    top, mass = merged(stats_ref[...])
-    lane = lax.broadcasted_iota(jnp.int32, out_ref.shape, 2)
-    out_ref[...] = jnp.where(lane == 0, top, mass)
+def stats_kernel(marginal_ref, out_ref):
+    marginal = marginal_ref[...]
+    best = jnp.max(jnp.max(marginal, axis=0, keepdims=True), axis=2, keepdims=True)
+    mass = jnp.sum(jnp.exp(marginal - best), axis=0, keepdims=True)
+    mass = jnp.sum(mass, axis=2, keepdims=True)
+    lane = lax.broadcasted_iota(jnp.int32, (1, 1, LANES), 2)
+    out_ref[...] = jnp.broadcast_to(jnp.where(lane == 0, best, mass), out_ref.shape)
 
 
 def final_kernel(stats_ref, marginal_ref, out_ref, evidence_ref, draws=0):
@@ -384,25 +381,23 @@
         ),
         *args, scratch=landing(args), pinned=True, flops=1 << 28, name="terms",
     )
-    marginal, stat = call(
+    marginal = call(
         functools.partial(score_kernel, zero=turned.index(0)),
-        (
-            jax.ShapeDtypeStruct((1, draws), F32),
-            jax.ShapeDtypeStruct((shards, 1, LANES), F32),
-        ),
+        jax.ShapeDtypeStruct((1, 1, draws), F32),
         everyone, *terms, flops=1 << 30, name="score",
     )
+    marginals = lax.all_gather(marginal, "bin", axis=0, tiled=True)
+    stat = call(
+        stats_kernel, jax.ShapeDtypeStruct((shards, 1, LANES), F32), marginals, name="stats"
+    )
     stats = lax.all_to_all(stat, "draw", 0, 0, axis_index_groups=[turned], tiled=True)
-    marginals = lax.all_gather(marginal.reshape(1, 1, draws), "bin", axis=0, tiled=True)
-    half = call(half_kernel, jax.ShapeDtypeStruct((1, 1, LANES), F32), stats, name="half")
-    halves = lax.all_gather(half, "bin", axis=0, tiled=True)
     weights, evidence = call(
         lambda *refs: final_kernel(*refs, draws=whole * shards),
         (
             jax.ShapeDtypeStruct((cores, 1, draws), F32),
             jax.ShapeDtypeStruct((1, 1), F32),
         ),
-        halves, marginals, name="final",
+        stats, marginals, name="final",
     )
     return weights.reshape(whole), evidence.reshape(1)
 

time: 85.5 us -> 82.9 us (0.970)
  blocking collectives: 10 us -> 28.7 us
  starting transfers between devices: 46.9 us -> 33 us
  waiting for transfers between devices: 18.1 us -> 11.3 us
    all_to_all x0 -> x1, blocking collectives: none -> 24.3 us  [body(): lax.all_to_all(stat, 'draw', 0, 0, axis_index_groups=[turned], tiled=True)]
    all_to_all x1 -> x0, starting transfers between devices: 13.9 us -> none  [body(): lax.all_to_all(stat, 'draw', 0, 0, axis_index_groups=[turned], tiled=True)]
    all_to_all x1 -> x0, waiting for transfers between devices: 6.72 us -> none  [body(): lax.all_to_all(stat, 'draw', 0, 0, axis_index_groups=[turned], tiled=True)]
    all_gather x2 -> x1, blocking collectives: 10 us -> 4.37 us  [body(): marginals = lax.all_gather(marginal, 'bin', axis=0, tiled=True)]
  transfers between devices with their start and end apart: 2 -> 1, of which waited for: 2 -> 1; matrix products, arithmetic and copies ran while one was open for 0% -> 0% of each run, Pallas kernels for 3% -> 3%
where the time goes in v5:
time: 82.9 us; the launch traced here: 82.5 us
  starting transfers between devices  33 us (40%)
  blocking collectives  28.7 us (35%)
  waiting for transfers between devices  11.3 us (14%)
  Pallas kernels  8.73 us (11%)
    all_to_all x1, starting transfers between devices, body(): lax.all_to_all(sums, 'draw', 0, 0, axis_index_groups=[turned], tiled=True)  33 us
    all_to_all x1, blocking collectives, body(): lax.all_to_all(stat, 'draw', 0, 0, axis_index_groups=[turned], tiled=True)  24.3 us
    all_to_all x1, waiting for transfers between devices, body(): lax.all_to_all(sums, 'draw', 0, 0, axis_index_groups=[turned], tiled=True)  11.3 us
    pallas_call x5, Pallas kernels, call(): pl.pallas_call(kernel, out_shape=outs, in_specs=[where] * len(args), out_...  8.73 us
    all_gather x1, blocking collectives, body(): marginals = lax.all_gather(marginal, 'bin', axis=0, tiled=True)  4.37 us
  transfers between devices with their start and end apart: 1, of which 1 were waited for; matrix products, arithmetic and copies ran while one was open for 0% of the time, Pallas kernels for 3%

profile of v5, /device:TPU:37, one launch (start us, length us, event | category | flops | bytes accessed | tf_op | source)
XLA Modules:
  0.0 82.5 jit_solution(17847286112154161250)
XLA Ops:
  0.6 2.3 %summary.1 = f32[32,1,456]{2,1,0:T(1,128)} custom-call(f32[3,2,256]{2,1,0:T(2,128)} %cross_in.1, f32[3,256]{1,0:T(4,128)} %power_in.1, s32[1,128]{1,0:T(1,128)} %bitcast.6), custom_call_target="tpu_custom_call" | custom-call | flops 16777216 | bytes 1048576 | tf_op jit(solution)/shard_map/summary/pallas_call | solution.py:61
  3.0 33.0 %all-to-all-start = ((f32[32,1,456]{2,1,0:T(1,128)}), f32[32,1,456]{2,1,0:T(1,128)S(1)}, u32[]{:S(2)}, u32[]{:S(2)}) async-start(f32[32,1,456]{2,1,0:T(1,128)} %summary.1), calls=%async_computation | async-start | bytes 131072 | tf_op jit(solution)/shard_map/all_to_all | solution.py:368
  36.0 2.8 %terms.1 = (bf16[1040,256]{1,0:T(8,128)(2,1)S(1)}, bf16[1040,256]{1,0:T(8,128)(2,1)S(1)}, f32[6,128,512]{2,1,0:T(8,128)S(1)}, f32[16,512]{1,0:T(8,128)S(1)}, s32[32,128]{1,0:T(8,128)S(1)}) custom-call(s32[1,128]{1,0:T(1,128)} %bitcast.7, f32[3,1024]{1,0:T(4,128)} %amps_in.1, f32[3,1024]{1,0:T(4,128)} %delays_in.1, f32[1,1024]{1,0:T(1,128)} %bitcast.8, ...), custom_call_target="tpu_custom_call" | custom-call | flops 268435456 | bytes 1048576 | tf_op jit(solution)/shard_map/terms/pallas_call | solution.py:61
  38.8 11.3 %all-to-all-done.sums_ref = f32[32,1,456]{2,1,0:T(1,128)S(1)} async-done(((f32[32,1,456]{2,1,0:T(1,128)}), f32[32,1,456]{2,1,0:T(1,128)S(1)}, u32[]{:S(2)}, u32[]{:S(2)}) %all-to-all-start) | async-done | bytes 58400 | tf_op jit(solution)/shard_map/all_to_all | solution.py:368
  50.1 2.6 %score.1 = f32[1,1,512]{2,1,0:T(1,128)S(1)} custom-call(f32[32,1,456]{2,1,0:T(1,128)S(1)} %all-to-all-done.sums_ref, bf16[1040,256]{1,0:T(8,128)(2,1)S(1)} %get-tuple-element.9.cos_ref, bf16[1040,256]{1,0:T(8,128)(2,1)S(1)} %get-tuple-element.10.sin_ref, f32[6,128,512]{2,1,0:T(8,128)S(1)} %get-tuple-element.11.features_ref, ...), custom_call_target="tpu_custom_call" | custom-call | flops 1073741824 | bytes 1048576 | tf_op jit(solution)/shard_map/score/pallas_call | solution.py:61
  52.7 4.4 %all_gather.3.marginal_ref.refs_1_ = f32[2,1,512]{2,1,0:T(1,128)S(1)} all-gather(f32[1,1,512]{2,1,0:T(1,128)S(1)} %score.1), channel_id=1, replica_groups=mesh['event'=4,'draw'=32,'bin'=2] {'bin'}, dimensions={0}, use_global_device_ids=true | all-gather | bytes 6144 | tf_op jit(solution)/shard_map/all_gather | solution.py:389
  57.1 0.2 stats.1
  57.3 24.3 %all_to_all.10.refs_0_ = f32[32,1,128]{2,1,0:T(1,128)S(1)} all-to-all(f32[32,1,128]{2,1,0:T(1,128)S(1)} %stats.1), channel_id=1, replica_groups={{48,50,52,54,56,58,60,62,0,2,4,6,8,10,12,14,16,18,20,22,24,26,28,30,32,..., dimensions={0} | all-to-all | bytes 32768 | tf_op jit(solution)/shard_map/all_to_all | solution.py:393
  81.6 0.9 %final.1 = (f32[2,1,512]{2,1,0:T(1,128)}, f32[1,1]{1,0:T(1,128)}) custom-call(f32[32,1,128]{2,1,0:T(1,128)S(1)} %all_to_all.10.refs_0_, f32[2,1,512]{2,1,0:T(1,128)S(1)} %all_gather.3.marginal_ref.refs_1_), custom_call_target="tpu_custom_call" | custom-call | flops 1048576 | bytes 1048576 | tf_op jit(solution)/shard_map/final/pallas_call | solution.py:61
Async XLA Ops:
  3.0 47.1 %all-to-all-start = ((f32[32,1,456]{2,1,0:T(1,128)}), f32[32,1,456]{2,1,0:T(1,128)S(1)}, u32[]{:S(2)}, u32[]{:S(2)}) async-start(f32[32,1,456]{2,1,0:T(1,128)} %summary.1), calls=%async_computation | async-start | bytes 131072 | tf_op jit(solution)/shard_map/all_to_all | solution.py:368

commit v6 on v5

--- a/solution.py
+++ b/solution.py
@@ -15,7 +15,8 @@
 WIDE = 256
 CHUNK = 128
 TAIL = 16
-STRIP = 128
+STRIP = 32
+LONG = 512
 LANES = 128
 DET = 3
 CHANNELS = 6
@@ -245,7 +246,8 @@
 
 
 def score_kernel(
-    sums_ref, cos_ref, sin_ref, features_ref, flat_ref, place_ref, out_ref, zero=0,
+    sums_ref, cos_ref, sin_ref, features_ref, flat_ref, place_ref, out_ref,
+    even_ref, odd_ref, zero=0,
 ):
     bins = features_ref.shape[1]
     draws = features_ref.shape[2]
@@ -308,7 +310,11 @@
         earliest = (even - odd)[:1]
         top = total = None
         for first in range(0, half, STRIP):
-            even, odd = rotated(slice(first, first + STRIP), columns)
+            if first % LONG == 0:
+                rows = slice(first, first + LONG)
+                even_ref[rows, columns], odd_ref[rows, columns] = rotated(rows, columns)
+            rows = slice(first, first + STRIP)
+            even, odd = even_ref[rows, columns], odd_ref[rows, columns]
             after, before = even + odd, even - odd
             if first == 0:
                 at = lax.broadcasted_iota(jnp.int32, before.shape, 0)
@@ -384,7 +390,7 @@
     marginal = call(
         functools.partial(score_kernel, zero=turned.index(0)),
         jax.ShapeDtypeStruct((1, 1, draws), F32),
-        everyone, *terms, flops=1 << 30, name="score",
+        everyone, *terms, scratch=[pltpu.VMEM((TSHIFT // 2, draws), F32)] * 2, flops=1 << 30, name="score",
     )
     marginals = lax.all_gather(marginal, "bin", axis=0, tiled=True)
     stat = call(

time: 82.9 us -> 82.9 us (level)
  no operation moved by 1% of the time
where the time goes in v6:
time: 82.9 us; the launch traced here: 82.4 us
  starting transfers between devices  33 us (40%)
  blocking collectives  28.7 us (35%)
  waiting for transfers between devices  11.3 us (14%)
  Pallas kernels  8.69 us (10%)
    all_to_all x1, starting transfers between devices, body(): lax.all_to_all(sums, 'draw', 0, 0, axis_index_groups=[turned], tiled=True)  33 us
    all_to_all x1, blocking collectives, body(): lax.all_to_all(stat, 'draw', 0, 0, axis_index_groups=[turned], tiled=True)  24.4 us
    all_to_all x1, waiting for transfers between devices, body(): lax.all_to_all(sums, 'draw', 0, 0, axis_index_groups=[turned], tiled=True)  11.3 us
    pallas_call x5, Pallas kernels, call(): pl.pallas_call(kernel, out_shape=outs, in_specs=[where] * len(args), out_...  8.69 us
    all_gather x1, blocking collectives, body(): marginals = lax.all_gather(marginal, 'bin', axis=0, tiled=True)  4.35 us
  transfers between devices with their start and end apart: 1, of which 1 were waited for; matrix products, arithmetic and copies ran while one was open for 0% of the time, Pallas kernels for 3%

profile of v6, /device:TPU:37, one launch (start us, length us, event | category | flops | bytes accessed | tf_op | source)
XLA Modules:
  0.0 82.4 jit_solution(16083137450055430203)
XLA Ops:
  0.6 2.3 %summary.1 = f32[32,1,456]{2,1,0:T(1,128)} custom-call(f32[3,2,256]{2,1,0:T(2,128)} %cross_in.1, f32[3,256]{1,0:T(4,128)} %power_in.1, s32[1,128]{1,0:T(1,128)} %bitcast.6), custom_call_target="tpu_custom_call" | custom-call | flops 16777216 | bytes 1048576 | tf_op jit(solution)/shard_map/summary/pallas_call | solution.py:62
  3.0 33.0 %all-to-all-start = ((f32[32,1,456]{2,1,0:T(1,128)}), f32[32,1,456]{2,1,0:T(1,128)S(1)}, u32[]{:S(2)}, u32[]{:S(2)}) async-start(f32[32,1,456]{2,1,0:T(1,128)} %summary.1), calls=%async_computation | async-start | bytes 131072 | tf_op jit(solution)/shard_map/all_to_all | solution.py:374
  36.0 2.8 %terms.1 = (bf16[1040,256]{1,0:T(8,128)(2,1)S(1)}, bf16[1040,256]{1,0:T(8,128)(2,1)S(1)}, f32[6,128,512]{2,1,0:T(8,128)S(1)}, f32[16,512]{1,0:T(8,128)S(1)}, s32[32,128]{1,0:T(8,128)S(1)}) custom-call(s32[1,128]{1,0:T(1,128)} %bitcast.7, f32[3,1024]{1,0:T(4,128)} %amps_in.1, f32[3,1024]{1,0:T(4,128)} %delays_in.1, f32[1,1024]{1,0:T(1,128)} %bitcast.8, ...), custom_call_target="tpu_custom_call" | custom-call | flops 268435456 | bytes 1048576 | tf_op jit(solution)/shard_map/terms/pallas_call | solution.py:62
  38.8 11.3 %all-to-all-done.sums_ref = f32[32,1,456]{2,1,0:T(1,128)S(1)} async-done(((f32[32,1,456]{2,1,0:T(1,128)}), f32[32,1,456]{2,1,0:T(1,128)S(1)}, u32[]{:S(2)}, u32[]{:S(2)}) %all-to-all-start) | async-done | bytes 58400 | tf_op jit(solution)/shard_map/all_to_all | solution.py:374
  50.1 2.6 %score.1 = f32[1,1,512]{2,1,0:T(1,128)S(1)} custom-call(f32[32,1,456]{2,1,0:T(1,128)S(1)} %all-to-all-done.sums_ref, bf16[1040,256]{1,0:T(8,128)(2,1)S(1)} %get-tuple-element.9.cos_ref, bf16[1040,256]{1,0:T(8,128)(2,1)S(1)} %get-tuple-element.10.sin_ref, f32[6,128,512]{2,1,0:T(8,128)S(1)} %get-tuple-element.11.features_ref, ...), custom_call_target="tpu_custom_call" | custom-call | flops 1073741824 | bytes 1048576 | tf_op jit(solution)/shard_map/score/pallas_call | solution.py:62
  52.7 4.4 %all_gather.3.marginal_ref.refs_1_ = f32[2,1,512]{2,1,0:T(1,128)S(1)} all-gather(f32[1,1,512]{2,1,0:T(1,128)S(1)} %score.1), channel_id=1, replica_groups=mesh['event'=4,'draw'=32,'bin'=2] {'bin'}, dimensions={0}, use_global_device_ids=true | all-gather | bytes 6144 | tf_op jit(solution)/shard_map/all_gather | solution.py:395
  57.0 0.2 stats.1
  57.2 24.4 %all_to_all.10.refs_0_ = f32[32,1,128]{2,1,0:T(1,128)S(1)} all-to-all(f32[32,1,128]{2,1,0:T(1,128)S(1)} %stats.1), channel_id=1, replica_groups={{48,50,52,54,56,58,60,62,0,2,4,6,8,10,12,14,16,18,20,22,24,26,28,30,32,..., dimensions={0} | all-to-all | bytes 32768 | tf_op jit(solution)/shard_map/all_to_all | solution.py:399
  81.6 0.9 %final.1 = (f32[2,1,512]{2,1,0:T(1,128)}, f32[1,1]{1,0:T(1,128)}) custom-call(f32[32,1,128]{2,1,0:T(1,128)S(1)} %all_to_all.10.refs_0_, f32[2,1,512]{2,1,0:T(1,128)S(1)} %all_gather.3.marginal_ref.refs_1_), custom_call_target="tpu_custom_call" | custom-call | flops 1048576 | bytes 1048576 | tf_op jit(solution)/shard_map/final/pallas_call | solution.py:62
Async XLA Ops:
  3.0 47.1 %all-to-all-start = ((f32[32,1,456]{2,1,0:T(1,128)}), f32[32,1,456]{2,1,0:T(1,128)S(1)}, u32[]{:S(2)}, u32[]{:S(2)}) async-start(f32[32,1,456]{2,1,0:T(1,128)} %summary.1), calls=%async_computation | async-start | bytes 131072 | tf_op jit(solution)/shard_map/all_to_all | solution.py:374

commit v7 on v5

--- a/solution.py
+++ b/solution.py
@@ -22,7 +22,7 @@
 SPAN = 68
 TERMS = 16
 PAYLOAD = CHANNELS * SPAN + DET * TERMS
-MEET = 0.75
+MEET = (0.75, 0.5)
 VMEM = pl.BlockSpec(memory_space=pltpu.VMEM)
 F32, BF16 = jnp.float32, jnp.bfloat16
 
@@ -358,7 +358,9 @@
     whole = log_amps.shape[1]
     draws = whole // cores
     widths = bin_widths.reshape(1, bins)
-    turned = [(i + int(shards * MEET)) % shards for i in range(shards)]
+    turned, late = (
+        [(i + int(shards * meet)) % shards for i in range(shards)] for meet in MEET
+    )
     args = (fine_cross, fine_power, widths)
     sums = call(
         functools.partial(summary_kernel, grid=float(fine * shards)),
@@ -390,7 +392,7 @@
     stat = call(
         stats_kernel, jax.ShapeDtypeStruct((shards, 1, LANES), F32), marginals, name="stats"
     )
-    stats = lax.all_to_all(stat, "draw", 0, 0, axis_index_groups=[turned], tiled=True)
+    stats = lax.all_to_all(stat, "draw", 0, 0, axis_index_groups=[late], tiled=True)
     weights, evidence = call(
         lambda *refs: final_kernel(*refs, draws=whole * shards),
         (

time: 82.9 us -> 82 us (0.989)
  blocking collectives: 28.7 us -> 27.7 us
    all_to_all x1, blocking collectives: 24.3 us -> 23.3 us  [body(): lax.all_to_all(stat, 'draw', 0, 0, axis_index_groups=[late], tiled=True)]
where the time goes in v7:
time: 82 us; the launch traced here: 81.4 us
  starting transfers between devices  33 us (40%)
  blocking collectives  27.7 us (34%)
  waiting for transfers between devices  11.3 us (14%)
  Pallas kernels  8.73 us (11%)
    all_to_all x1, starting transfers between devices, body(): lax.all_to_all(sums, 'draw', 0, 0, axis_index_groups=[turned], tiled=True)  33 us
    all_to_all x1, blocking collectives, body(): lax.all_to_all(stat, 'draw', 0, 0, axis_index_groups=[late], tiled=True)  23.3 us
    all_to_all x1, waiting for transfers between devices, body(): lax.all_to_all(sums, 'draw', 0, 0, axis_index_groups=[turned], tiled=True)  11.3 us
    pallas_call x5, Pallas kernels, call(): pl.pallas_call(kernel, out_shape=outs, in_specs=[where] * len(args), out_...  8.73 us
    all_gather x1, blocking collectives, body(): marginals = lax.all_gather(marginal, 'bin', axis=0, tiled=True)  4.37 us
  transfers between devices with their start and end apart: 1, of which 1 were waited for; matrix products, arithmetic and copies ran while one was open for 0% of the time, Pallas kernels for 3%

profile of v7, /device:TPU:37, one launch (start us, length us, event | category | flops | bytes accessed | tf_op | source)
XLA Modules:
  0.0 81.4 jit_solution(16706087699657942064)
XLA Ops:
  0.6 2.3 %summary.1 = f32[32,1,456]{2,1,0:T(1,128)} custom-call(f32[3,2,256]{2,1,0:T(2,128)} %cross_in.1, f32[3,256]{1,0:T(4,128)} %power_in.1, s32[1,128]{1,0:T(1,128)} %bitcast.6), custom_call_target="tpu_custom_call" | custom-call | flops 16777216 | bytes 1048576 | tf_op jit(solution)/shard_map/summary/pallas_call | solution.py:61
  3.0 33.0 %all-to-all-start = ((f32[32,1,456]{2,1,0:T(1,128)}), f32[32,1,456]{2,1,0:T(1,128)S(1)}, u32[]{:S(2)}, u32[]{:S(2)}) async-start(f32[32,1,456]{2,1,0:T(1,128)} %summary.1), calls=%async_computation | async-start | bytes 131072 | tf_op jit(solution)/shard_map/all_to_all | solution.py:370
  36.0 2.8 %terms.1 = (bf16[1040,256]{1,0:T(8,128)(2,1)S(1)}, bf16[1040,256]{1,0:T(8,128)(2,1)S(1)}, f32[6,128,512]{2,1,0:T(8,128)S(1)}, f32[16,512]{1,0:T(8,128)S(1)}, s32[32,128]{1,0:T(8,128)S(1)}) custom-call(s32[1,128]{1,0:T(1,128)} %bitcast.7, f32[3,1024]{1,0:T(4,128)} %amps_in.1, f32[3,1024]{1,0:T(4,128)} %delays_in.1, f32[1,1024]{1,0:T(1,128)} %bitcast.8, ...), custom_call_target="tpu_custom_call" | custom-call | flops 268435456 | bytes 1048576 | tf_op jit(solution)/shard_map/terms/pallas_call | solution.py:61
  38.8 11.3 %all-to-all-done.sums_ref = f32[32,1,456]{2,1,0:T(1,128)S(1)} async-done(((f32[32,1,456]{2,1,0:T(1,128)}), f32[32,1,456]{2,1,0:T(1,128)S(1)}, u32[]{:S(2)}, u32[]{:S(2)}) %all-to-all-start) | async-done | bytes 58400 | tf_op jit(solution)/shard_map/all_to_all | solution.py:370
  50.1 2.6 %score.1 = f32[1,1,512]{2,1,0:T(1,128)S(1)} custom-call(f32[32,1,456]{2,1,0:T(1,128)S(1)} %all-to-all-done.sums_ref, bf16[1040,256]{1,0:T(8,128)(2,1)S(1)} %get-tuple-element.9.cos_ref, bf16[1040,256]{1,0:T(8,128)(2,1)S(1)} %get-tuple-element.10.sin_ref, f32[6,128,512]{2,1,0:T(8,128)S(1)} %get-tuple-element.11.features_ref, ...), custom_call_target="tpu_custom_call" | custom-call | flops 1073741824 | bytes 1048576 | tf_op jit(solution)/shard_map/score/pallas_call | solution.py:61
  52.7 4.4 %all_gather.3.marginal_ref.refs_1_ = f32[2,1,512]{2,1,0:T(1,128)S(1)} all-gather(f32[1,1,512]{2,1,0:T(1,128)S(1)} %score.1), channel_id=1, replica_groups=mesh['event'=4,'draw'=32,'bin'=2] {'bin'}, dimensions={0}, use_global_device_ids=true | all-gather | bytes 6144 | tf_op jit(solution)/shard_map/all_gather | solution.py:391
  57.1 0.2 stats.1
  57.3 23.3 %all_to_all.10.refs_0_ = f32[32,1,128]{2,1,0:T(1,128)S(1)} all-to-all(f32[32,1,128]{2,1,0:T(1,128)S(1)} %stats.1), channel_id=1, replica_groups={{32,34,36,38,40,42,44,46,48,50,52,54,56,58,60,62,0,2,4,6,8,10,12,14,16,..., dimensions={0} | all-to-all | bytes 32768 | tf_op jit(solution)/shard_map/all_to_all | solution.py:395
  80.6 0.9 %final.1 = (f32[2,1,512]{2,1,0:T(1,128)}, f32[1,1]{1,0:T(1,128)}) custom-call(f32[32,1,128]{2,1,0:T(1,128)S(1)} %all_to_all.10.refs_0_, f32[2,1,512]{2,1,0:T(1,128)S(1)} %all_gather.3.marginal_ref.refs_1_), custom_call_target="tpu_custom_call" | custom-call | flops 1048576 | bytes 1048576 | tf_op jit(solution)/shard_map/final/pallas_call | solution.py:61
Async XLA Ops:
  3.0 47.1 %all-to-all-start = ((f32[32,1,456]{2,1,0:T(1,128)}), f32[32,1,456]{2,1,0:T(1,128)S(1)}, u32[]{:S(2)}, u32[]{:S(2)}) async-start(f32[32,1,456]{2,1,0:T(1,128)} %summary.1), calls=%async_computation | async-start | bytes 131072 | tf_op jit(solution)/shard_map/all_to_all | solution.py:370

commit v8 on v7

--- a/solution.py
+++ b/solution.py
@@ -130,10 +130,10 @@
 def summary_kernel(
     cross_in, power_in, widths_in, out_ref, cross_ref, power_ref, widths_ref, sems, grid=0.0
 ):
-    for copy in fetch(
+    copies = fetch(
         (widths_in, cross_in, power_in), (widths_ref, cross_ref, power_ref), sems
-    ):
-        copy.wait()
+    )
+    copies[0].wait()
     fine, bins = power_ref.shape[1], widths_ref.shape[1]
     wide, upper = edges(widths_ref[...])
     lower = upper - wide
@@ -144,6 +144,8 @@
     down = jnp.where(inside, 2.0 * wide - up, 0.0)
     both_high, both_low = split(up * down)
     weights = jnp.concatenate([up.astype(BF16), down.astype(BF16), both_high, both_low], axis=1)
+    for copy in copies[1:]:
+        copy.wait()
     data = jnp.concatenate(
         [cross_ref[d] for d in range(DET)] + [power_ref[...], jnp.zeros((7, fine), F32)], axis=0
     )

time: 82 us -> 82 us (level)
  no operation moved by 1% of the time
where the time goes in v8:
time: 82 us; the launch traced here: 81.4 us
  starting transfers between devices  33 us (40%)
  blocking collectives  27.7 us (34%)
  waiting for transfers between devices  11.3 us (14%)
  Pallas kernels  8.72 us (11%)
    all_to_all x1, starting transfers between devices, body(): lax.all_to_all(sums, 'draw', 0, 0, axis_index_groups=[turned], tiled=True)  33 us
    all_to_all x1, blocking collectives, body(): lax.all_to_all(stat, 'draw', 0, 0, axis_index_groups=[late], tiled=True)  23.3 us
    all_to_all x1, waiting for transfers between devices, body(): lax.all_to_all(sums, 'draw', 0, 0, axis_index_groups=[turned], tiled=True)  11.3 us
    pallas_call x5, Pallas kernels, call(): pl.pallas_call(kernel, out_shape=outs, in_specs=[where] * len(args), out_...  8.72 us
    all_gather x1, blocking collectives, body(): marginals = lax.all_gather(marginal, 'bin', axis=0, tiled=True)  4.36 us
  transfers between devices with their start and end apart: 1, of which 1 were waited for; matrix products, arithmetic and copies ran while one was open for 0% of the time, Pallas kernels for 3%

profile of v8, /device:TPU:37, one launch (start us, length us, event | category | flops | bytes accessed | tf_op | source)
XLA Modules:
  0.0 81.4 jit_solution(8306256798094054706)
XLA Ops:
  0.6 2.3 %summary.1 = f32[32,1,456]{2,1,0:T(1,128)} custom-call(f32[3,2,256]{2,1,0:T(2,128)} %cross_in.1, f32[3,256]{1,0:T(4,128)} %power_in.1, s32[1,128]{1,0:T(1,128)} %bitcast.6), custom_call_target="tpu_custom_call" | custom-call | flops 16777216 | bytes 1048576 | tf_op jit(solution)/shard_map/summary/pallas_call | solution.py:61
  2.9 33.0 %all-to-all-start = ((f32[32,1,456]{2,1,0:T(1,128)}), f32[32,1,456]{2,1,0:T(1,128)S(1)}, u32[]{:S(2)}, u32[]{:S(2)}) async-start(f32[32,1,456]{2,1,0:T(1,128)} %summary.1), calls=%async_computation | async-start | bytes 131072 | tf_op jit(solution)/shard_map/all_to_all | solution.py:372
  36.0 2.8 %terms.1 = (bf16[1040,256]{1,0:T(8,128)(2,1)S(1)}, bf16[1040,256]{1,0:T(8,128)(2,1)S(1)}, f32[6,128,512]{2,1,0:T(8,128)S(1)}, f32[16,512]{1,0:T(8,128)S(1)}, s32[32,128]{1,0:T(8,128)S(1)}) custom-call(s32[1,128]{1,0:T(1,128)} %bitcast.7, f32[3,1024]{1,0:T(4,128)} %amps_in.1, f32[3,1024]{1,0:T(4,128)} %delays_in.1, f32[1,1024]{1,0:T(1,128)} %bitcast.8, ...), custom_call_target="tpu_custom_call" | custom-call | flops 268435456 | bytes 1048576 | tf_op jit(solution)/shard_map/terms/pallas_call | solution.py:61
  38.8 11.3 %all-to-all-done.sums_ref = f32[32,1,456]{2,1,0:T(1,128)S(1)} async-done(((f32[32,1,456]{2,1,0:T(1,128)}), f32[32,1,456]{2,1,0:T(1,128)S(1)}, u32[]{:S(2)}, u32[]{:S(2)}) %all-to-all-start) | async-done | bytes 58400 | tf_op jit(solution)/shard_map/all_to_all | solution.py:372
  50.1 2.6 %score.1 = f32[1,1,512]{2,1,0:T(1,128)S(1)} custom-call(f32[32,1,456]{2,1,0:T(1,128)S(1)} %all-to-all-done.sums_ref, bf16[1040,256]{1,0:T(8,128)(2,1)S(1)} %get-tuple-element.9.cos_ref, bf16[1040,256]{1,0:T(8,128)(2,1)S(1)} %get-tuple-element.10.sin_ref, f32[6,128,512]{2,1,0:T(8,128)S(1)} %get-tuple-element.11.features_ref, ...), custom_call_target="tpu_custom_call" | custom-call | flops 1073741824 | bytes 1048576 | tf_op jit(solution)/shard_map/score/pallas_call | solution.py:61
  52.7 4.4 %all_gather.3.marginal_ref.refs_1_ = f32[2,1,512]{2,1,0:T(1,128)S(1)} all-gather(f32[1,1,512]{2,1,0:T(1,128)S(1)} %score.1), channel_id=1, replica_groups=mesh['event'=4,'draw'=32,'bin'=2] {'bin'}, dimensions={0}, use_global_device_ids=true | all-gather | bytes 6144 | tf_op jit(solution)/shard_map/all_gather | solution.py:393
  57.1 0.2 stats.1
  57.2 23.3 %all_to_all.10.refs_0_ = f32[32,1,128]{2,1,0:T(1,128)S(1)} all-to-all(f32[32,1,128]{2,1,0:T(1,128)S(1)} %stats.1), channel_id=1, replica_groups={{32,34,36,38,40,42,44,46,48,50,52,54,56,58,60,62,0,2,4,6,8,10,12,14,16,..., dimensions={0} | all-to-all | bytes 32768 | tf_op jit(solution)/shard_map/all_to_all | solution.py:397
  80.6 0.9 %final.1 = (f32[2,1,512]{2,1,0:T(1,128)}, f32[1,1]{1,0:T(1,128)}) custom-call(f32[32,1,128]{2,1,0:T(1,128)S(1)} %all_to_all.10.refs_0_, f32[2,1,512]{2,1,0:T(1,128)S(1)} %all_gather.3.marginal_ref.refs_1_), custom_call_target="tpu_custom_call" | custom-call | flops 1048576 | bytes 1048576 | tf_op jit(solution)/shard_map/final/pallas_call | solution.py:61
Async XLA Ops:
  2.9 47.1 %all-to-all-start = ((f32[32,1,456]{2,1,0:T(1,128)}), f32[32,1,456]{2,1,0:T(1,128)S(1)}, u32[]{:S(2)}, u32[]{:S(2)}) async-start(f32[32,1,456]{2,1,0:T(1,128)} %summary.1), calls=%async_computation | async-start | bytes 131072 | tf_op jit(solution)/shard_map/all_to_all | solution.py:372
